TPU v7x, 256 devices: a whole 4x4x8 slice. The times are simulated.
256 devices in a mesh: gx: 4 (over x), gy: 8 (over z), gz: 8 (over y, core).
Axes of the slice: x: 4, y: 4, z: 8, core: 2. Of those that a mesh axis runs over, the one named last changes fastest.
Arguments:
- right_side: float32 [128, 256, 1024], P('gx', 'gy', 'gz'), may hold values from -1 to 1
- z_faces: float32 [1024], P('gz'), may hold values from 0.5 to 2, as said below
- xy_coupling: float32 [5], replicated, as said below
- block_inverse: float32 [5, 1024, 128], P(None, 'gz'), as said below
Outputs:
- solution: float32 [128, 256, 1024], P('gx', 'gy', 'gz')
- residual: float32 [128, 256, 1024], P('gx', 'gy', 'gz')
Inputs may be any that keep to these rules, and one draw needn't show every extreme that they name: z_faces is positive. xy_coupling[l] lies between 2.9 * 4^-l / 128^2 and 5.5 * 4^-l / 128^2. block_inverse[l] holds, block by block, the inverses of the 128 x 128 diagonal blocks of M_l built from z_faces and xy_coupling[l].
All inputs are finite; a program needn't handle non-finite values.
Results may differ from a plain program's by a relative error of at most 0.028.
Values sent between devices are 32-bit elements; how exact they have to be, the bound alone decides.
A program may use at most 128 MiB of HBM per device.

v0:
```python
import math

import jax
import jax.numpy as jnp
from jax import lax
from jax.sharding import PartitionSpec as P

LEVELS = 5
SWEEPS = 2


damping = 0.8
highest = lax.Precision.HIGHEST


def joined_along(pieces, dim):
    dims = list(pieces.shape[1:])
    dims[dim] *= pieces.shape[0]
    return jnp.moveaxis(pieces, 0, dim).reshape(dims)


def copy_for_each(value, axis):
    size = lax.axis_size(axis)
    return lax.all_to_all(
        jnp.broadcast_to(value[None], (size, *value.shape)), axis, 0, 0, tiled=True
    )


def gather_directly(value, axis, dim):
    return joined_along(copy_for_each(value, axis), dim)


def extended(value, sides, width):
    edges = {}
    for axis, dim in sides:
        size, length = (lax.axis_size(axis), value.shape[dim])
        up = [(i, (i + 1) % size) for i in range(size - 1)]
        last = lax.slice_in_dim(value, length - width, length, axis=dim)
        initial = lax.slice_in_dim(value, 0, width, axis=dim)
        edges[dim] = (
            lax.ppermute(last, axis, up),
            lax.ppermute(initial, axis, [(b, a) for a, b in up]),
        )
    done = []
    for _, dim in sides:
        low, high = edges[dim]
        around = [(width, width) if d in done else (0, 0) for d in range(value.ndim)]
        value = jnp.concatenate([jnp.pad(low, around), value, jnp.pad(high, around)], axis=dim)
        done.append(dim)
    return value


def side_by_side(arrays, axis, dim, along):
    widths = [math.prod(a.shape[along:]) for a in arrays]
    both = jnp.concatenate(
        [a.reshape(*a.shape[:along], w) for a, w in zip(arrays, widths)], axis=along
    )
    whole = lax.all_gather(both, axis, axis=dim, tiled=True)
    pieces = jnp.split(whole, [sum(widths[:k]) for k in range(1, len(widths))], axis=along)
    return tuple(
        (b.reshape(*whole.shape[:along], *a.shape[along:]) for a, b in zip(arrays, pieces))
    )


def extended_2(cells, sides, width):
    for axis, dim in sides:
        count = lax.axis_size(axis)
        ends = count - 1
        head = lax.slice_in_dim(cells, 0, width, axis=dim)
        tail = lax.slice_in_dim(cells, cells.shape[dim] - width, cells.shape[dim], axis=dim)
        cells = jnp.concatenate(
            [
                lax.ppermute(tail, axis, [(i, (i + 1) % count) for i in range(ends)]),
                cells,
                lax.ppermute(head, axis, [((i + 1) % count, i) for i in range(ends)]),
            ],
            axis=dim,
        )
    return cells


def interface_setup(corner_aa, corner_ab, corner_ba, corner_bb, couplings):
    determinant = corner_aa * corner_bb - corner_ab * corner_ba
    corner_inverse = (
        jnp.stack(
            [jnp.stack([corner_bb, -corner_ab], -1), jnp.stack([-corner_ba, corner_aa], -1)], -2
        )
        / determinant[:, None, None]
    )
    blocks_count = corner_aa.shape[0]
    identity = jnp.eye(blocks_count, dtype=corner_inverse.dtype)
    diagonal_part = jnp.einsum("kab,kl->kalb", corner_inverse, identity, precision=highest).reshape(
        2 * blocks_count, 2 * blocks_count
    )
    link_values = jnp.zeros((2 * blocks_count - 1,), corner_inverse.dtype).at[1::2].set(-couplings)
    schur_matrix = diagonal_part + jnp.diag(link_values, 1) + jnp.diag(link_values, -1)
    return (corner_inverse, diagonal_part, jnp.linalg.cholesky(schur_matrix))


def make_solver(inverse_block, corner_rows, couplings, device_index, down_coupling, up_coupling):
    corner_inverse, diagonal_part, factor = interface_setup(
        corner_rows[:, 0], corner_rows[:, 1], corner_rows[:, 2], corner_rows[:, 3], couplings
    )
    block_len = inverse_block.shape[0]
    forward = lax.linalg.triangular_solve(factor, diagonal_part, left_side=True, lower=True)
    reach = lax.linalg.triangular_solve(
        factor, forward, left_side=True, lower=True, transpose_a=True
    )
    padded_reach = jnp.pad(reach, ((1, 1), (0, 0)))
    slice_rows = lax.dynamic_slice_in_dim(padded_reach, 2 * device_index, 4, 0)
    needed = jnp.stack([slice_rows[0], slice_rows[3]])

    def neighbours(end_values):
        zero_carry = jnp.zeros(end_values.shape, jnp.float32)
        nearby = zero_carry + jnp.dot(
            needed, gather_directly(end_values, "gz", 0), precision=highest
        )
        return (nearby[0], nearby[1])

    def solve(source):
        first_extent, second_extent, depth = source.shape
        line_count = first_extent * second_extent
        local_part = jnp.einsum("xyj,ij->xyi", source, inverse_block, precision=highest)
        end_values = jnp.stack(
            [
                local_part[:, :, 0].reshape(line_count),
                local_part[:, :, block_len - 1].reshape(line_count),
            ]
        )
        below_last, above_first = neighbours(end_values)
        return (
            local_part
            + (down_coupling * below_last).reshape(first_extent, second_extent, 1)
            * inverse_block[:, 0]
            + (up_coupling * above_first).reshape(first_extent, second_extent, 1)
            * inverse_block[:, block_len - 1]
        )

    return solve


def apply_operator(iterate, lateral_weight, down_faces, up_faces):
    padded = extended(iterate, (("gx", 0), ("gy", 1), ("gz", 2)), 1)
    lateral = (
        padded[:-2, 1:-1, 1:-1]
        + padded[2:, 1:-1, 1:-1]
        + padded[1:-1, :-2, 1:-1]
        + padded[1:-1, 2:, 1:-1]
    )
    return (
        lateral_weight * (4.0 * iterate - lateral)
        + down_faces * (iterate - padded[1:-1, 1:-1, :-2])
        + up_faces * (iterate - padded[1:-1, 1:-1, 2:])
    )


def restrict(field):
    first_extent, second_extent, depth = field.shape
    return field.reshape(first_extent // 2, 2, second_extent // 2, 2, depth).sum(axis=(1, 3)) * 0.25


def prolong(padded):
    first_extent = padded.shape[0] - 2
    second_extent = padded.shape[1] - 2
    depth = padded.shape[2]
    even_rows = 0.75 * padded[1:-1] + 0.25 * padded[:-2]
    odd_rows = 0.75 * padded[1:-1] + 0.25 * padded[2:]
    widened = jnp.stack([even_rows, odd_rows], 1).reshape(
        2 * first_extent, second_extent + 2, depth
    )
    even_rows = 0.75 * widened[:, 1:-1] + 0.25 * widened[:, :-2]
    odd_rows = 0.75 * widened[:, 1:-1] + 0.25 * widened[:, 2:]
    return jnp.stack([even_rows, odd_rows], 2).reshape(2 * first_extent, 2 * second_extent, depth)


def body(right_side, z_faces, xy_coupling, block_inverse):
    device_index = lax.axis_index("gz")
    levels_count = block_inverse.shape[0]
    last_cell = block_inverse.shape[1] - 1
    corner = jnp.stack(
        [
            block_inverse[:, 0, 0],
            block_inverse[:, 0, last_cell],
            block_inverse[:, last_cell, 0],
            block_inverse[:, last_cell, last_cell],
        ],
        -1,
    )[None]
    corners, firsts = side_by_side((corner, z_faces[:1]), "gz", 0, 1)
    couplings = firsts[1:]
    edge_faces = jnp.concatenate([firsts, jnp.ones((1,), jnp.float32)])
    top_face = lax.dynamic_slice_in_dim(edge_faces, device_index + 1, 1, 0)
    up_faces = jnp.concatenate([z_faces[1:], top_face])
    solvers = [
        make_solver(
            block_inverse[level],
            corners[:, level],
            couplings,
            device_index,
            z_faces[0],
            top_face[0],
        )
        for level in range(levels_count)
    ]

    def operator(iterate, level):
        return apply_operator(iterate, xy_coupling[level], z_faces, up_faces)

    def multigrid_cycle(source, level):
        iterate = damping * solvers[level](source)
        iterate = iterate + damping * solvers[level](source - operator(iterate, level))
        if level == LEVELS - 1:
            return iterate
        coarse = multigrid_cycle(restrict(source - operator(iterate, level)), level + 1)
        widened = extended_2(coarse, (("gx", 0), ("gy", 1)), 1)
        iterate = iterate + prolong(widened)
        for sweep in range(SWEEPS):
            iterate = iterate + damping * solvers[level](source - operator(iterate, level))
        return iterate

    solution = multigrid_cycle(right_side, 0)
    return (solution, right_side - operator(solution, 0))


def solution(mesh):
    return jax.shard_map(
        body,
        mesh=mesh,
        in_specs=(P("gx", "gy", "gz"), P("gz"), P(), P(None, "gz", None)),
        out_specs=(P("gx", "gy", "gz"), P("gx", "gy", "gz")),
        check_vma=False,
    )
```

profile of v0, /device:TPU:2, one launch (start us, length us, event | category | flops | bytes accessed | tf_op | source)
XLA Modules:
  0.0 704.7 jit_solution(5164038338720317318)
XLA Ops:
  9.1 11.0 %all-gather = f32[8,1,21]{2,1,0:T(1,128)S(1)} all-gather(f32[1,1,21]{2,1,0:T(1,128)S(1)} %maximum_bitcast_fusion.10), channel_id=1, replica_groups=mesh['gx'=4,'gy'=8,'gz'=8] {'gz'}, dimensions={0}, use_global_device_ids=true | all-gather | bytes 756 | tf_op jit(solution)/shard_map/all_gather | solution.py:58
  63.7 9.3 %all-to-all-start.1 = ((f32[8,2,1024]{2,1,0:T(2,128)}), f32[8,2,1024]{2,1,0:T(2,128)S(1)}, u32[]{:S(2)}, u32[]{:S(2)}) async-start(f32[8,2,1024]{2,1,0:T(2,128)} %broadcast_in_dim.111), calls=%async_computation.1 | async-start | bytes 131072 | tf_op jit(solution)/shard_map/all_to_all | solution.py:24
  101.1 10.1 %all-to-all-start.2 = ((f32[8,2,256]{2,1,0:T(2,128)}), f32[8,2,256]{2,1,0:T(2,128)S(1)}, u32[]{:S(2)}, u32[]{:S(2)}) async-start(f32[8,2,256]{2,1,0:T(2,128)} %broadcast_in_dim.112), calls=%async_computation.2 | async-start | bytes 32768 | tf_op jit(solution)/shard_map/all_to_all | solution.py:24
  137.1 6.5 all-to-all-start.3
  170.7 6.3 all-to-all-start.4
  184.7 5.8 collective-permute-start.26
  255.5 5.8 collective-permute-start.38
  269.3 10.3 %all_to_all.90 = f32[8,2,16]{2,1,0:T(2,128)S(1)} all-to-all(f32[8,2,16]{2,1,0:T(2,128)S(1)} %broadcast_in_dim.117), channel_id=1, replica_groups=mesh['gx'=4,'gy'=8,'gz'=8] {'gz'}, dimensions={0} | all-to-all | bytes 2048 | tf_op jit(solution)/shard_map/all_to_all | solution.py:24
  286.6 5.8 collective-permute-start.44
  318.4 5.8 collective-permute-start.50
  332.1 10.2 %all_to_all.91 = f32[8,2,4]{2,1,0:T(2,128)S(1)} all-to-all(f32[8,2,4]{2,1,0:T(2,128)S(1)} %broadcast_in_dim.119), channel_id=1, replica_groups=mesh['gx'=4,'gy'=8,'gz'=8] {'gz'}, dimensions={0} | all-to-all | bytes 512 | tf_op jit(solution)/shard_map/all_to_all | solution.py:24
  352.4 5.8 collective-permute-start.56
  384.0 10.3 %all_to_all.92 = f32[8,2,16]{2,1,0:T(2,128)S(1)} all-to-all(f32[8,2,16]{2,1,0:T(2,128)S(1)} %broadcast_in_dim.120), channel_id=1, replica_groups=mesh['gx'=4,'gy'=8,'gz'=8] {'gz'}, dimensions={0} | all-to-all | bytes 2048 | tf_op jit(solution)/shard_map/all_to_all | solution.py:24
  401.2 5.8 collective-permute-start.66
  415.0 10.3 %all_to_all.93 = f32[8,2,16]{2,1,0:T(2,128)S(1)} all-to-all(f32[8,2,16]{2,1,0:T(2,128)S(1)} %broadcast_in_dim.121), channel_id=1, replica_groups=mesh['gx'=4,'gy'=8,'gz'=8] {'gz'}, dimensions={0} | all-to-all | bytes 2048 | tf_op jit(solution)/shard_map/all_to_all | solution.py:24
  434.9 5.8 collective-permute-start.72
  464.1 10.7 %all_to_all.94 = f32[8,1,128]{2,1,0:T(1,128)S(1)} all-to-all(f32[8,1,128]{2,1,0:T(1,128)S(1)} %reshape.906), channel_id=1, replica_groups=mesh['gx'=4,'gy'=8,'gz'=8] {'gz'}, dimensions={0} | all-to-all | bytes 8192 | tf_op jit(solution)/shard_map/all_to_all | solution.py:24
  495.5 10.5 %all_to_all.95 = f32[8,1,128]{2,1,0:T(1,128)S(1)} all-to-all(f32[8,1,128]{2,1,0:T(1,128)S(1)} %reshape.908), channel_id=1, replica_groups=mesh['gx'=4,'gy'=8,'gz'=8] {'gz'}, dimensions={0} | all-to-all | bytes 8192 | tf_op jit(solution)/shard_map/all_to_all | solution.py:24
  515.3 5.8 collective-permute-start.88
  545.0 11.7 %all_to_all.96 = f32[8,2,256]{2,1,0:T(2,128)S(1)} all-to-all(f32[8,2,256]{2,1,0:T(2,128)S(1)} %broadcast_in_dim.124), channel_id=1, replica_groups=mesh['gx'=4,'gy'=8,'gz'=8] {'gz'}, dimensions={0} | all-to-all | bytes 32768 | tf_op jit(solution)/shard_map/all_to_all | solution.py:24
  576.9 11.6 %all_to_all.97 = f32[8,2,256]{2,1,0:T(2,128)S(1)} all-to-all(f32[8,2,256]{2,1,0:T(2,128)S(1)} %broadcast_in_dim.125), channel_id=1, replica_groups=mesh['gx'=4,'gy'=8,'gz'=8] {'gz'}, dimensions={0} | all-to-all | bytes 32768 | tf_op jit(solution)/shard_map/all_to_all | solution.py:24
  597.2 5.8 collective-permute-start.104
  629.1 15.6 %all_to_all.98 = f32[8,2,1024]{2,1,0:T(2,128)S(1)} all-to-all(f32[8,2,1024]{2,1,0:T(2,128)S(1)} %broadcast_in_dim.126), channel_id=1, replica_groups=mesh['gx'=4,'gy'=8,'gz'=8] {'gz'}, dimensions={0} | all-to-all | bytes 131072 | tf_op jit(solution)/shard_map/all_to_all | solution.py:24
  666.6 15.6 %all_to_all.99 = f32[8,2,1024]{2,1,0:T(2,128)S(1)} all-to-all(f32[8,2,1024]{2,1,0:T(2,128)S(1)} %broadcast_in_dim.127), channel_id=1, replica_groups=mesh['gx'=4,'gy'=8,'gz'=8] {'gz'}, dimensions={0} | all-to-all | bytes 131072 | tf_op jit(solution)/shard_map/all_to_all | solution.py:24
  (740 shorter events, 489.2 us)
Async XLA Ops:
  3.6 39.0 %all-to-all-start = ((f32[8,2,1024]{2,1,0:T(2,128)}), f32[8,2,1024]{2,1,0:T(2,128)S(1)}, u32[]{:S(2)}, u32[]{:S(2)}) async-start(f32[8,2,1024]{2,1,0:T(2,128)} %broadcast_in_dim.110), calls=%async_computation | async-start | bytes 131072 | tf_op jit(solution)/shard_map/all_to_all | solution.py:24
  63.7 14.9 %all-to-all-start.1 = ((f32[8,2,1024]{2,1,0:T(2,128)}), f32[8,2,1024]{2,1,0:T(2,128)S(1)}, u32[]{:S(2)}, u32[]{:S(2)}) async-start(f32[8,2,1024]{2,1,0:T(2,128)} %broadcast_in_dim.111), calls=%async_computation.1 | async-start | bytes 131072 | tf_op jit(solution)/shard_map/all_to_all | solution.py:24
  101.1 15.5 %all-to-all-start.2 = ((f32[8,2,256]{2,1,0:T(2,128)}), f32[8,2,256]{2,1,0:T(2,128)S(1)}, u32[]{:S(2)}, u32[]{:S(2)}) async-start(f32[8,2,256]{2,1,0:T(2,128)} %broadcast_in_dim.112), calls=%async_computation.2 | async-start | bytes 32768 | tf_op jit(solution)/shard_map/all_to_all | solution.py:24
  184.7 14.2 %collective-permute-start.26 = (f32[8,1,128]{2,1,0:T(1,128)S(1)}, f32[8,1,128]{2,1,0:T(1,128)S(1)}, u32[]{:S(2)}, u32[]{:S(2)}) collective-permute-start(f32[8,1,128]{2,1,0:T(1,128)S(1)} %get-tuple-element.190), channel_id=1, source_target_pairs={{0,8},{8,16},{16,24},{24,32},{32,40},{40,48},{48,56},{1,9},{9,17},... | collective-permute-start | bytes 12296 | tf_op jit(solution)/shard_map/ppermute | solution.py:41
  217.5 14.2 %collective-permute-start.32 = (f32[8,1,128]{2,1,0:T(1,128)S(1)}, f32[8,1,128]{2,1,0:T(1,128)S(1)}, u32[]{:S(2)}, u32[]{:S(2)}) collective-permute-start(f32[8,1,128]{2,1,0:T(1,128)S(1)} %get-tuple-element.184), channel_id=1, source_target_pairs={{0,8},{8,16},{16,24},{24,32},{32,40},{40,48},{48,56},{1,9},{9,17},... | collective-permute-start | bytes 12296 | tf_op jit(solution)/shard_map/ppermute | solution.py:41
  249.7 18.3 %collective-permute-start.36 = (f32[1,4,128]{2,1,0:T(4,128)S(1)}, f32[1,4,128]{2,1,0:T(4,128)S(1)}, u32[]{:S(2)}, u32[]{:S(2)}) collective-permute-start(f32[1,4,128]{2,1,0:T(4,128)S(1)} %get-tuple-element.231), channel_id=1, source_target_pairs={{0,64},{64,128},{128,192},{1,65},{65,129},{129,193},{2,66},{66,130... | collective-permute-start | bytes 6152 | tf_op jit(solution)/shard_map/ppermute | solution.py:41
  253.1 14.9 %collective-permute-start.37 = (f32[1,4,128]{2,1,0:T(4,128)S(1)}, f32[1,4,128]{2,1,0:T(4,128)S(1)}, u32[]{:S(2)}, u32[]{:S(2)}) collective-permute-start(f32[1,4,128]{2,1,0:T(4,128)S(1)} %get-tuple-element.232), channel_id=1, source_target_pairs={{64,0},{128,64},{192,128},{65,1},{129,65},{193,129},{66,2},{130,66... | collective-permute-start | bytes 6152 | tf_op jit(solution)/shard_map/ppermute | solution.py:42
  280.7 18.3 %collective-permute-start.42 = (f32[1,4,128]{2,1,0:T(4,128)S(1)}, f32[1,4,128]{2,1,0:T(4,128)S(1)}, u32[]{:S(2)}, u32[]{:S(2)}) collective-permute-start(f32[1,4,128]{2,1,0:T(4,128)S(1)} %get-tuple-element.225), channel_id=1, source_target_pairs={{0,64},{64,128},{128,192},{1,65},{65,129},{129,193},{2,66},{66,130... | collective-permute-start | bytes 6152 | tf_op jit(solution)/shard_map/ppermute | solution.py:41
  284.2 14.9 %collective-permute-start.43 = (f32[1,4,128]{2,1,0:T(4,128)S(1)}, f32[1,4,128]{2,1,0:T(4,128)S(1)}, u32[]{:S(2)}, u32[]{:S(2)}) collective-permute-start(f32[1,4,128]{2,1,0:T(4,128)S(1)} %get-tuple-element.226), channel_id=1, source_target_pairs={{64,0},{128,64},{192,128},{65,1},{129,65},{193,129},{66,2},{130,66... | collective-permute-start | bytes 6152 | tf_op jit(solution)/shard_map/ppermute | solution.py:42
  312.5 18.3 %collective-permute-start.48 = (f32[1,2,128]{2,1,0:T(2,128)S(1)}, f32[1,2,128]{2,1,0:T(2,128)S(1)}, u32[]{:S(2)}, u32[]{:S(2)}) collective-permute-start(f32[1,2,128]{2,1,0:T(2,128)S(1)} %get-tuple-element.254), channel_id=1, source_target_pairs={{0,64},{64,128},{128,192},{1,65},{65,129},{129,193},{2,66},{66,130... | collective-permute-start | bytes 3080 | tf_op jit(solution)/shard_map/ppermute | solution.py:41
  316.0 14.9 %collective-permute-start.49 = (f32[1,2,128]{2,1,0:T(2,128)S(1)}, f32[1,2,128]{2,1,0:T(2,128)S(1)}, u32[]{:S(2)}, u32[]{:S(2)}) collective-permute-start(f32[1,2,128]{2,1,0:T(2,128)S(1)} %get-tuple-element.255), channel_id=1, source_target_pairs={{64,0},{128,64},{192,128},{65,1},{129,65},{193,129},{66,2},{130,66... | collective-permute-start | bytes 3080 | tf_op jit(solution)/shard_map/ppermute | solution.py:42
  365.0 17.7 %collective-permute-start.58 = (f32[1,4,128]{2,1,0:T(4,128)S(1)}, f32[1,4,128]{2,1,0:T(4,128)S(1)}, u32[]{:S(2)}, u32[]{:S(2)}) collective-permute-start(f32[1,4,128]{2,1,0:T(4,128)S(1)} %get-tuple-element.213), channel_id=1, source_target_pairs={{0,64},{64,128},{128,192},{1,65},{65,129},{129,193},{2,66},{66,130... | collective-permute-start | bytes 6152 | tf_op jit(solution)/shard_map/ppermute | solution.py:41
  368.1 14.7 %collective-permute-start.59 = (f32[1,4,128]{2,1,0:T(4,128)S(1)}, f32[1,4,128]{2,1,0:T(4,128)S(1)}, u32[]{:S(2)}, u32[]{:S(2)}) collective-permute-start(f32[1,4,128]{2,1,0:T(4,128)S(1)} %get-tuple-element.214), channel_id=1, source_target_pairs={{64,0},{128,64},{192,128},{65,1},{129,65},{193,129},{66,2},{130,66... | collective-permute-start | bytes 6152 | tf_op jit(solution)/shard_map/ppermute | solution.py:42
  395.4 18.3 %collective-permute-start.64 = (f32[1,4,128]{2,1,0:T(4,128)S(1)}, f32[1,4,128]{2,1,0:T(4,128)S(1)}, u32[]{:S(2)}, u32[]{:S(2)}) collective-permute-start(f32[1,4,128]{2,1,0:T(4,128)S(1)} %get-tuple-element.207), channel_id=1, source_target_pairs={{0,64},{64,128},{128,192},{1,65},{65,129},{129,193},{2,66},{66,130... | collective-permute-start | bytes 6152 | tf_op jit(solution)/shard_map/ppermute | solution.py:41
  398.4 15.3 %collective-permute-start.65 = (f32[1,4,128]{2,1,0:T(4,128)S(1)}, f32[1,4,128]{2,1,0:T(4,128)S(1)}, u32[]{:S(2)}, u32[]{:S(2)}) collective-permute-start(f32[1,4,128]{2,1,0:T(4,128)S(1)} %get-tuple-element.208), channel_id=1, source_target_pairs={{64,0},{128,64},{192,128},{65,1},{129,65},{193,129},{66,2},{130,66... | collective-permute-start | bytes 6152 | tf_op jit(solution)/shard_map/ppermute | solution.py:42
  446.4 16.4 %collective-permute-start.74 = (f32[1,8,128]{2,1,0:T(8,128)S(1)}, f32[1,8,128]{2,1,0:T(8,128)S(1)}, u32[]{:S(2)}, u32[]{:S(2)}) collective-permute-start(f32[1,8,128]{2,1,0:T(8,128)S(1)} %get-tuple-element.176), channel_id=1, source_target_pairs={{0,64},{64,128},{128,192},{1,65},{65,129},{129,193},{2,66},{66,130... | collective-permute-start | bytes 12296 | tf_op jit(solution)/shard_map/ppermute | solution.py:41
  448.3 14.4 %collective-permute-start.75 = (f32[1,8,128]{2,1,0:T(8,128)S(1)}, f32[1,8,128]{2,1,0:T(8,128)S(1)}, u32[]{:S(2)}, u32[]{:S(2)}) collective-permute-start(f32[1,8,128]{2,1,0:T(8,128)S(1)} %get-tuple-element.177), channel_id=1, source_target_pairs={{64,0},{128,64},{192,128},{65,1},{129,65},{193,129},{66,2},{130,66... | collective-permute-start | bytes 12296 | tf_op jit(solution)/shard_map/ppermute | solution.py:42
  476.6 17.6 %collective-permute-start.80 = (f32[1,8,128]{2,1,0:T(8,128)S(1)}, f32[1,8,128]{2,1,0:T(8,128)S(1)}, u32[]{:S(2)}, u32[]{:S(2)}) collective-permute-start(f32[1,8,128]{2,1,0:T(8,128)S(1)} %get-tuple-element.170), channel_id=1, source_target_pairs={{0,64},{64,128},{128,192},{1,65},{65,129},{129,193},{2,66},{66,130... | collective-permute-start | bytes 12296 | tf_op jit(solution)/shard_map/ppermute | solution.py:41
  478.5 15.7 %collective-permute-start.81 = (f32[1,8,128]{2,1,0:T(8,128)S(1)}, f32[1,8,128]{2,1,0:T(8,128)S(1)}, u32[]{:S(2)}, u32[]{:S(2)}) collective-permute-start(f32[1,8,128]{2,1,0:T(8,128)S(1)} %get-tuple-element.171), channel_id=1, source_target_pairs={{64,0},{128,64},{192,128},{65,1},{129,65},{193,129},{66,2},{130,66... | collective-permute-start | bytes 12296 | tf_op jit(solution)/shard_map/ppermute | solution.py:42
  526.9 16.5 %collective-permute-start.90 = (f32[1,16,128]{2,1,0:T(8,128)S(1)}, f32[1,16,128]{2,1,0:T(8,128)S(1)}, u32[]{:S(2)}, u32[]{:S(2)}) collective-permute-start(f32[1,16,128]{2,1,0:T(8,128)S(1)} %get-tuple-element.144), channel_id=1, source_target_pairs={{0,64},{64,128},{128,192},{1,65},{65,129},{129,193},{2,66},{66,130... | collective-permute-start | bytes 24584 | tf_op jit(solution)/shard_map/ppermute | solution.py:41
  528.9 14.6 %collective-permute-start.91 = (f32[1,16,128]{2,1,0:T(8,128)S(1)}, f32[1,16,128]{2,1,0:T(8,128)S(1)}, u32[]{:S(2)}, u32[]{:S(2)}) collective-permute-start(f32[1,16,128]{2,1,0:T(8,128)S(1)} %get-tuple-element.145), channel_id=1, source_target_pairs={{64,0},{128,64},{192,128},{65,1},{129,65},{193,129},{66,2},{130,66... | collective-permute-start | bytes 24584 | tf_op jit(solution)/shard_map/ppermute | solution.py:42
  557.8 17.6 %collective-permute-start.96 = (f32[1,16,128]{2,1,0:T(8,128)S(1)}, f32[1,16,128]{2,1,0:T(8,128)S(1)}, u32[]{:S(2)}, u32[]{:S(2)}) collective-permute-start(f32[1,16,128]{2,1,0:T(8,128)S(1)} %get-tuple-element.138), channel_id=1, source_target_pairs={{0,64},{64,128},{128,192},{1,65},{65,129},{129,193},{2,66},{66,130... | collective-permute-start | bytes 24584 | tf_op jit(solution)/shard_map/ppermute | solution.py:41
  559.7 15.7 %collective-permute-start.97 = (f32[1,16,128]{2,1,0:T(8,128)S(1)}, f32[1,16,128]{2,1,0:T(8,128)S(1)}, u32[]{:S(2)}, u32[]{:S(2)}) collective-permute-start(f32[1,16,128]{2,1,0:T(8,128)S(1)} %get-tuple-element.139), channel_id=1, source_target_pairs={{64,0},{128,64},{192,128},{65,1},{129,65},{193,129},{66,2},{130,66... | collective-permute-start | bytes 24584 | tf_op jit(solution)/shard_map/ppermute | solution.py:42
  683.7 14.5 %collective-permute-start.120 = (f32[32,1,128]{2,1,0:T(1,128)S(1)}, f32[32,1,128]{2,1,0:T(1,128)S(1)}, u32[]{:S(2)}, u32[]{:S(2)}) collective-permute-start(f32[32,1,128]{2,1,0:T(1,128)S(1)} %get-tuple-element.97), channel_id=1, source_target_pairs={{0,8},{8,16},{16,24},{24,32},{32,40},{40,48},{48,56},{1,9},{9,17},... | collective-permute-start | bytes 49160 | tf_op jit(solution)/shard_map/ppermute | solution.py:41
  (113 other events, 829.8 us)
where the time goes:
time: 718 us; the launch traced here: 705 us
  starting transfers between devices  370 us (52%)
  blocking collectives  128 us (18%)
  waiting for transfers between devices  108 us (15%)
  other arithmetic  46.6 us (6%)
  local copies, waits for them, and re-layouts  26.5 us (4%)
  matrix products  21.8 us (3%)
    ppermute x54, starting transfers between devices, extended(): lax.ppermute(last, axis, up)  164 us
    all_to_all x10, blocking collectives, copy_for_each(): lax.all_to_all(jnp.broadcast_to(value[None], (size, *value.shape)), axis,...  117 us
    ppermute x54, starting transfers between devices, extended(): lax.ppermute(initial, axis, [(b, a) for a, b in up])  101 us
    all_to_all x8, starting transfers between devices, copy_for_each(): lax.all_to_all(jnp.broadcast_to(value[None], (size, *value.shape)), axis,...  52.5 us
    ppermute x54, waiting for transfers between devices, extended(): lax.ppermute(initial, axis, [(b, a) for a, b in up])  46.7 us
    all_to_all x8, waiting for transfers between devices, copy_for_each(): lax.all_to_all(jnp.broadcast_to(value[None], (size, *value.shape)), axis,...  34.3 us
    ppermute x8, starting transfers between devices, extended_2(): lax.ppermute(tail, axis, [(i, (i + 1) % count) for i in range(ends)])  33.4 us
    ppermute x8, waiting for transfers between devices, extended_2(): lax.ppermute(head, axis, [((i + 1) % count, i) for i in range(ends)])  26.9 us
  transfers between devices with their start and end apart: 132, of which 40 were waited for; matrix products, arithmetic and copies ran while one was open for 4% of the time, Pallas kernels for 0%

commit v1 on v0

v1 whole, which is shorter than its diff:
```python
import jax
import jax.numpy as jnp
from jax import lax
from jax.experimental import pallas as pl
from jax.experimental.pallas import tpu as pltpu
from jax.sharding import PartitionSpec as P

f32 = jnp.float32
bf16 = jnp.bfloat16
HI = lax.Precision.HIGHEST
MESH = pl.DeviceIdType.MESH
DIRS = [(dx, dy) for dx in (-1, 0, 1) for dy in (-1, 0, 1) if (dx, dy) != (0, 0)]

LX = [32, 16, 8, 4, 2]
OX = [4, 3, 3, 4, 4]
OY = [8, 8, 8, 4, 4]
SX = [40, 22, 14, 12, 10]
SY = [48, 32, 24, 16, 16]


def pair_of(p):
    if p < 12:
        return p // 4 + 1, p % 4 + 1
    return (0 if p < 14 else 4), p % 2 + 1


def pid(l, m):
    if l == 0:
        return 11 + m
    if l == 4:
        return 13 + m
    return (l - 1) * 4 + m - 1


def split(x):
    h = x.astype(bf16)
    return h, (x - h.astype(f32)).astype(bf16)


def mm(a, b, trans_b=False):
    dims = (((1,), (1 if trans_b else 0,)), ((), ()))
    return lax.dot_general(a, b, dims, preferred_element_type=f32)


def dot3(a, b, trans_b=False):
    ah, al = split(a)
    bh, bl = split(b)
    return mm(ah, bh, trans_b) + (mm(ah, bl, trans_b) + mm(al, bh, trans_b))


def hdot(a, b):
    return jnp.dot(a, b, precision=HI, preferred_element_type=f32)


def iota(shape, dim):
    return lax.broadcasted_iota(jnp.int32, shape, dim)


def scratch_shapes():
    out = {}
    for l in range(5):
        out[f"S{l}"] = (2, SX[l], SY[l], 128)
        for t in ("TA", "TB", "TC", "AA", "BB", "CC", "MA", "P0", "P1", "P2"):
            out[f"{t}{l}"] = (2, SX[l], SY[l], 128)
        if l:
            for t in ("M", "U", "V"):
                out[f"{t}{l}"] = (2, SX[l], SY[l], 128)
    out["fb3"] = out["mb3"] = (2, 4, 8, 128)
    out["fb4"] = out["mb4"] = (2, 2, 8, 128)
    out["rb3"] = out["qb3"] = (8, 2, 4, 8, 128)
    out["rb4"] = out["qb4"] = (8, 2, 2, 8, 128)
    out["rows"] = (4, 16, 128)
    out["re0"] = (8, 128)
    out["re1"] = (32, 128)
    out["cg"] = (9, 16, 128)
    out["cgl"] = (16, 128)
    out["e0"] = (8, 8, 1920)
    out["e1"] = (8, 32, 256)
    out["el0"] = (8, 1920)
    out["el1"] = (32, 256)
    return out


def kernel(sizes, f_ref, zf_ref, g_ref, e_ref, sol_ref, res_ref, *refs):
    names = list(scratch_shapes())
    r_ = dict(zip(names, refs))
    th, tl, hs, hr, gs, gr = refs[len(names):]
    S0, S1, S2, S3, S4 = [r_[f"S{l}"] for l in range(5)]
    M1, M2, M3, M4 = [r_[f"M{l}"] for l in range(1, 5)]
    fb3, fb4, mb3, mb4 = r_["fb3"], r_["fb4"], r_["mb3"], r_["mb4"]
    rb3, rb4, qb3, qb4 = r_["rb3"], r_["rb4"], r_["qb3"], r_["qb4"]
    rows, re0, re1, cg, cgl = r_["rows"], r_["re0"], r_["re1"], r_["cg"], r_["cgl"]
    e0, e1, el0, el1 = r_["e0"], r_["e1"], r_["el0"], r_["el1"]

    ngx, ngy, ngz = sizes
    ix, iy, k = lax.axis_index("gx"), lax.axis_index("gy"), lax.axis_index("gz")
    S = [S0, S1, S2, S3, S4]
    M = [None, M1, M2, M3, M4]

    def at(name, l):
        return r_[f"{name}{l}"]


    def peer(o):
        return jnp.where(k + o >= ngz, k + o - ngz, k + o)

    def exists(dx, dy):
        x, y = ix + dx, iy + dy
        return (x >= 0) & (x < ngx) & (y >= 0) & (y < ngy)

    def clear(ref):
        def step(i, c):
            ref[i] = jnp.zeros(ref.shape[1:], f32)
            return c
        lax.fori_loop(0, ref.shape[0], step, 0)

    def clear2(ref):
        def step(i, c):
            for h in range(2):
                ref[h, i] = jnp.zeros(ref.shape[2:], f32)
            return c
        lax.fori_loop(0, ref.shape[1], step, 0)

    for r in (S0, S1, S2, S3, S4, M1, M2, M3, M4):
        clear2(r)
    for r in (cg, e0, e1, rb3, rb4, qb3, qb4, fb3, fb4, mb3, mb4, rows):
        clear(r)

    barrier = pltpu.get_barrier_semaphore()
    count = jnp.int32(ngz - 1)
    for dx, dy in DIRS:
        ok = exists(dx, dy)

        @pl.when(ok)
        def _():
            pl.semaphore_signal(
                barrier, inc=1, device_id=(ix + dx, iy + dy, k), device_id_type=MESH
            )

        count = count + jnp.where(ok, 1, 0)
    for o in range(1, ngz):
        pl.semaphore_signal(
            barrier, inc=1, device_id=(ix, iy, peer(o)), device_id_type=MESH
        )

    def exchange(phase, pick):
        def copy(d, dx, dy):
            src, dst = pick(dx, dy)
            return pltpu.make_async_remote_copy(
                src_ref=src, dst_ref=dst, send_sem=hs.at[phase, d], recv_sem=hr.at[phase, d],
                device_id=(ix + dx, iy + dy, k), device_id_type=MESH,
            )

        def start():
            for d, (dx, dy) in enumerate(DIRS):
                @pl.when(exists(dx, dy))
                def _():
                    copy(d, dx, dy).start()

        def wait_recv():
            for d, (dx, dy) in enumerate(DIRS):
                @pl.when(exists(-dx, -dy))
                def _():
                    copy(d, dx, dy).wait_recv()

        def wait_send():
            for d, (dx, dy) in enumerate(DIRS):
                @pl.when(exists(dx, dy))
                def _():
                    copy(d, dx, dy).wait_send()

        return start, wait_recv, wait_send

    def span(d, off, n, h):
        if d == 0:
            return pl.ds(off, n), pl.ds(off, n)
        if d == 1:
            return pl.ds(off + n - h, h), pl.ds(off - h, h)
        return pl.ds(off, h), pl.ds(off + n, h)

    def halo(phase, buf, half, ox, n, hx):
        def pick(dx, dy):
            sx, tx = span(dx, ox, n, hx)
            sy, ty = span(dy, 8, n, 8)
            if half is None:
                return buf.at[:, sx, sy, :], buf.at[:, tx, ty, :]
            return buf.at[half, sx, sy, :], buf.at[half, tx, ty, :]
        return exchange(phase, pick)

    def whole(phase, blk, rbuf):
        def pick(dx, dy):
            return blk, rbuf.at[DIRS.index((dx, dy))]
        return exchange(phase, pick)

    def gather(phase, src, buf):
        def copy(o):
            return pltpu.make_async_remote_copy(
                src_ref=src, dst_ref=buf.at[k], send_sem=gs.at[phase, o],
                recv_sem=gr.at[phase, o], device_id=(ix, iy, peer(o)),
                device_id_type=MESH,
            )

        def start():
            for o in range(1, ngz):
                copy(o).start()

        def wait_recv():
            for o in range(1, ngz):
                copy(o).wait_recv()

        def wait_send():
            for o in range(1, ngz):
                copy(o).wait_send()

        return start, wait_recv, wait_send

    sends = []

    a = [4.0 * e_ref[l] for l in range(5)]
    for l in range(5):
        rows[0, 2 * l : 2 * l + 1, :] = a[l] * g_ref[l, 0:1, :]
        rows[0, 2 * l + 1 : 2 * l + 2, :] = a[l] * g_ref[l, 127:128, :]
    for m in range(1, 4):
        prev = rows[m - 1]
        for l in range(5):
            nxt = a[l] * hdot(prev, g_ref[l])
            rows[m, 2 * l : 2 * l + 2, :] = nxt[2 * l : 2 * l + 2]
    for m in range(4):
        re0[2 * m : 2 * m + 2, :] = rows[m, 0:2, :]
    for p in range(16):
        l, m = pair_of(p)
        re1[2 * p : 2 * p + 2, :] = rows[m - 1, 2 * l : 2 * l + 2, :]
    lane16 = iota((16, 128), 1)
    tile = jnp.where(lane16 == 8, jnp.broadcast_to(zf_ref[0:1, 0:1], (16, 128)), 0.0)
    for n in range(4):
        rn = rows[n]
        tile = jnp.where(lane16 == 2 * n, jnp.broadcast_to(rn[:, 0:1], (16, 128)), tile)
        tile = jnp.where(lane16 == 2 * n + 1, jnp.broadcast_to(rn[:, 127:128], (16, 128)), tile)
    cgl[...] = tile
    cg[k] = tile

    def put_f(i, c):
        S0[0, 4 + i, 8:40, :] = f_ref[i]
        return c
    lax.fori_loop(0, 32, put_f, 0)

    pl.semaphore_wait(barrier, count)

    c_start, c_recv, c_send = gather(0, cgl, cg)
    c_start()

    def pick0(dx, dy):
        sx, tx = span(dx, 4, 32, 4)
        sy, ty = span(dy, 8, 32, 8)
        sx0, _ = span(dx, 0, 32, 4)
        sy0, _ = span(dy, 0, 32, 8)
        return f_ref.at[sx0, sy0, :], S0.at[0, tx, ty, :]

    h_start, h_recv, h_send = exchange(0, pick0)
    h_start()
    sends += [c_send, h_send]

    h_recv()
    r0 = re0[...]
    for i in range(5):
        fx = S0[0, 8 * i : 8 * i + 8].reshape(384, 128)
        el0[:, 384 * i : 384 * i + 384] = dot3(r0, fx, True)
    e0[k] = el0[...]
    g0_start, g0_recv, g0_send = gather(1, el0, e0)
    g0_start()
    sends.append(g0_send)

    c_recv()
    CG = cg[0:8].reshape(128, 128)
    ri, ci = iota((128, 128), 0), iota((128, 128), 1)
    same = (ri >> 1) == (ci >> 1)
    odd = (ci & 1) == 1
    eye = jnp.where(ri == ci, 1.0, 0.0).astype(f32)

    def col(c):
        return jnp.broadcast_to(CG[:, c : c + 1], (128, 128))

    def corner(n):
        return jnp.where(same, jnp.where(odd, col(2 * n + 1), col(2 * n)), 0.0)

    lrow = (ri >> 1) & 7
    inva = jnp.zeros((128, 128), f32)
    for l in range(5):
        inva = jnp.where(lrow == l, 1.0 / a[l], inva)
    face = col(8)
    face_up = jnp.concatenate([face[16:], jnp.zeros((16, 128), f32)], 0)
    K = inva * (
        jnp.where(((ri & 1) == 0) & (ci == ri - 15), face, 0.0)
        + jnp.where(((ri & 1) == 1) & (ci == ri + 15), face_up, 0.0)
    )
    R = corner(0)
    blk = (ri >> 4) + (ri & 1)
    for st in (1, 2, 4):
        link = jnp.where((blk & (2 * st - 1)) == st, K, 0.0)
        d = R * eye
        drow = jnp.sum(d, 1, keepdims=True)
        dcol = jnp.sum(d, 0, keepdims=True)
        off = link / (1.0 - link * link * drow * dcol)
        diag = jnp.sum(off * link * dcol, 1, keepdims=True)
        R = R + hdot(hdot(R, off + eye * diag), R)
    W = eye + hdot(R, K)
    B2, B3, B4 = dot3(corner(1), K), dot3(corner(2), K), dot3(corner(3), K)
    V1 = dot3(W, dot3(B2, W))
    V2 = dot3(W, dot3(B3, W) + dot3(B2, V1))
    V3 = dot3(W, dot3(B4, W) + dot3(B3, V1) + dot3(B2, V2))
    VS = [W, V1, V2, V3]

    def lm_of(p):
        l = jnp.where(p < 12, (p >> 2) + 1, jnp.where(p < 14, 0, 4))
        m = jnp.where(p < 12, (p & 3) + 1, (p & 1) + 1)
        return l, m

    def funct(level):
        width = 64 if level == 0 else 256
        rr, rc = iota((128, 128), 0), iota((128, 128), 1)
        p, side = rr & 15, rr >> 4
        if level == 0:
            l, m = jnp.zeros_like(p), p - 11
            live = (rr < 32) & (p >= 12)
        else:
            l, m = lm_of(p)
            live = rr < 32
        target = jnp.where(side == 0, (k - 1) * 16 + l * 2 + 1, (k + 1) * 16 + l * 2)
        pick_rows = jnp.where(live & (rc == target), 1.0, 0.0).astype(f32)
        er, ec = iota((128, width), 0), iota((128, width), 1)
        if level == 0:
            jc, lc, mc, endc = ec >> 3, jnp.zeros_like(ec), ((ec >> 1) & 3) + 1, ec & 1
        else:
            jc, endc = ec >> 5, ec & 1
            lc, mc = lm_of((ec >> 1) & 15)
        expand = jnp.where(er == jc * 16 + lc * 2 + endc, 1.0, 0.0).astype(f32)
        wr = iota((128, width), 0)
        mrow = ((wr & 15) - 11) if level == 0 else lm_of(wr & 15)[1]
        out = jnp.zeros((128, width), f32)
        for n in range(4):
            x = dot3(dot3(pick_rows, VS[n]), expand)
            out = out + jnp.where(mrow - mc == n, x, 0.0)
        return out

    L0 = funct(0)
    L1 = funct(1)

    side_in, side_out = ri >> 4, ci >> 4
    pi, po = ri & 15, ci & 15
    fl = (ri < 32) & (ci < 32) & (side_in == side_out)
    li, mi = lm_of(pi)
    lo, mo = lm_of(po)
    aout = jnp.zeros((128, 128), f32)
    for l in range(5):
        aout = jnp.where(lo == l, a[l], aout)
    cm = jnp.broadcast_to(zf_ref[0:1, 0:1], (1, 128))
    cp = jnp.broadcast_to(cg[k + 1, 0:1, 8:9], (1, 128))
    for l in range(5):
        gt = g_ref[l].T
        p1 = pid(l, 1)
        ut = jnp.where(ri == p1, jnp.broadcast_to(cm * gt[0:1], (128, 128)), 0.0)
        ut = jnp.where(ri == 16 + p1, jnp.broadcast_to(cp * gt[127:128], (128, 128)), ut)
        if l == 0:
            q = jnp.where(fl & (pi >= 13) & (pi == po + 1), 1.0, 0.0)
        else:
            den = jnp.where(lo == l, 1.0, a[l] - aout)
            amp = a[l] / den
            nb = -aout / den
            p2 = nb * nb
            p3 = p2 * nb
            dm = mo - mi
            pw = jnp.where(dm == 0, 1.0, jnp.where(dm == 1, nb, jnp.where(dm == 2, p2, p3)))
            pm = jnp.where(mo == 1, nb, jnp.where(mo == 2, p2, jnp.where(mo == 3, p3, p2 * p2)))
            q = jnp.where((li == lo) & (dm >= 0), amp * pw, 0.0)
            q = q + jnp.where((li == l) & (mi == 1), pm, 0.0)
            q = jnp.where(lo == l, jnp.where((li == l) & (mi == mo + 1), 1.0, 0.0), q)
            q = jnp.where(fl, q, 0.0)
        for r, v in ((0, a[l] * gt), (128, ut)):
            vh, vl = split(v)
            th[l, r : r + 128, 0:128] = vh
            tl[l, r : r + 128, 0:128] = vl
        qh, ql = split(q.astype(f32))
        zero = jnp.zeros((128, 128), bf16)
        th[l, 0:128, 128:256] = zero
        tl[l, 0:128, 128:256] = zero
        th[l, 128:256, 128:256] = qh
        tl[l, 128:256, 128:256] = ql

    def apply(l, src, dst, step, n, scale=None):
        y = src.shape[2]

        def body(i, c):
            x = pl.ds(i * step, step)
            v = jnp.concatenate(
                [src[0, x].reshape(step * y, 128), src[1, x].reshape(step * y, 128)], 1
            )
            vh, vl = split(v)
            t = mm(vh, th[l]) + (mm(vh, tl[l]) + mm(vl, th[l]))
            if scale is not None:
                t = scale * t
            dst[0, x] = t[:, 0:128].reshape(step, y, 128)
            dst[1, x] = t[:, 128:256].reshape(step, y, 128)
            return c

        lax.fori_loop(0, n, body, 0)

    def stencil(l, src, dst, grow, post, halves=(0, 1)):
        ox, oy, n, y = OX[l], OY[l], LX[l], SY[l]
        gy0 = iota((y, 128), 0) + (iy * n - oy)
        ym = jnp.where((gy0 >= 0) & (gy0 < ngy * n), 0.25, 0.0).astype(f32)

        def body(x, c):
            gx0 = ix * n + x - ox
            s = jnp.where((gx0 >= 0) & (gx0 < ngx * n), 1.0, 0.0).astype(f32)
            m4 = ym * s
            for h in halves:
                v = src[h, x]
                t = (src[h, x - 1] + src[h, x + 1]) + (
                    pltpu.roll(v, 1, 0) + pltpu.roll(v, y - 1, 0)
                )
                dst(h, x, post(h, x, m4 * t))
            return c

        lax.fori_loop(ox - grow, ox + n + grow, body, 0)

    def into(ref):
        def put(h, x, v):
            ref[h, x] = v
        return put

    def solve(l, src, dst, matrix=None, scale=None):
        step, n = (8, 5) if l == 0 else (SX[l], 1)
        apply(l if matrix is None else matrix, src, dst, step, n, scale)

    def residual(l, halves=(0, 1)):
        s, ta, tb = S[l], at("TA", l), at("TB", l)
        aa, bb = at("AA", l), at("BB", l)
        solve(l, s, ta)
        solve(l, ta, tb)
        stencil(l, tb, into(bb), 1, lambda h, x, v: 0.32 * ta[h, x] + 0.64 * v, halves)
        stencil(l, bb, into(aa), 0, lambda h, x, v: 0.04 * s[h, x] + v, halves)

    def smoothed(l):
        w = 1 if l == 0 else 0
        s, ta, tb, tc = S[l], at("TA", l), at("TB", l), at("TC", l)
        bb, cc, ma = at("BB", l), at("CC", l), at("MA", l)
        solve(l, tb, tc)
        stencil(l, tc, into(bb), 2 + w, lambda h, x, v: 0.8192 * tb[h, x] + 0.4096 * v)
        stencil(l, bb, into(cc), 1 + w, lambda h, x, v: 0.9728 * ta[h, x] + v)
        stencil(l, cc, into(ma), w, lambda h, x, v: 0.9984 * s[h, x] + v)

    def restrict(l, put, halves=(0, 1)):
        ox, oy, n = OX[l], OY[l], LX[l] // 2
        aa = at("AA", l)

        def body(i, c):
            x = ox + 2 * i
            for h in halves:
                even, off = pl.ds(oy, n, 2), pl.ds(oy + 1, n, 2)
                v = (aa[h, x, even, :] + aa[h, x, off, :]) + (
                    aa[h, x + 1, even, :] + aa[h, x + 1, off, :]
                )
                put(h, i, 0.25 * v)
            return c

        lax.fori_loop(0, n, body, 0)

    def unpack(dst, blk, rbuf, n):
        for h in range(2):
            for i in range(n):
                dst[h, 4 + i, 4 : 4 + n, :] = blk[h, i, 0:n, :]
                for d, (dx, dy) in enumerate(DIRS):
                    dst[h, 4 - n * dx + i, 4 - n * dy : 4 - n * dy + n, :] = rbuf[d, h, i, 0:n, :]

    def correct(l, store):
        c = l + 1
        w = 1 if l == 0 else 0
        m, u, g2 = M[c], at("U", c), at("V", c)
        kap = a[l] / a[c]
        solve(c, m, u, c, kap)
        solve(c, u, g2, l, 0.64)
        q = 0.04 * (1.0 - a[c] / a[l])
        n, ox, oc = LX[c], OX[l], OX[c]
        y = SY[c]
        ys, cnt = [(4, 24), (4, 16), (0, 12), (2, 8)][l]
        gyc = iota((cnt, 128), 0) + (iy * n + ys - OY[c])
        ym = jnp.where((gyc >= 0) & (gyc < ngy * n), 1.0, 0.0).astype(f32)
        outs = [at("P0", l), at("P1", l), at("P2", l)]

        def fields(h, x):
            uv = u[h, x]
            return (0.04 * m[h, x] + q * uv, 0.32 * uv, g2[h, x])

        def body(j, carry):
            j = j - (1 + w)
            gx = ix * n + j
            s = jnp.where((gx >= 0) & (gx < ngx * n), 1.0, 0.0).astype(f32)
            ms = ym * s
            for h in range(2):
                lower, here, upper = (fields(h, oc + j + i) for i in (-1, 0, 1))
                for o, lo_, he, up_ in zip(outs, lower, here, upper):
                    for i, far in enumerate((lo_, up_)):
                        v = 0.75 * he + 0.25 * far
                        ev = (0.75 * v + 0.25 * pltpu.roll(v, 1, 0))[ys : ys + cnt]
                        od = (0.75 * v + 0.25 * pltpu.roll(v, y - 1, 0))[ys : ys + cnt]
                        o[h, ox + 2 * j + i, pl.ds(0, cnt, 2), :] = ms * ev
                        o[h, ox + 2 * j + i, pl.ds(1, cnt, 2), :] = ms * od
            return carry

        lax.fori_loop(0, n + 2 + 2 * w, body, 0)
        cc, ma = at("CC", l), at("MA", l)
        stencil(l, outs[2], into(cc), 1 + w, lambda h, x, v: outs[1][h, x] + v)
        stencil(l, cc, store, w, lambda h, x, v: (ma[h, x] + outs[0][h, x]) + v)

    g0_recv()
    for i in range(5):
        phi = dot3(L0, e0[:, :, 384 * i : 384 * i + 384].reshape(64, 384))
        S0[1, 8 * i : 8 * i + 8] = phi.T.reshape(8, 48, 128)
    residual(0, (0,))

    def put1(h, i, v):
        S1[h, 3 + i, 8:24, :] = v
    restrict(0, put1, (0,))
    x1_start, x1_recv, x1_send = halo(1, S1, 0, 3, 16, 3)
    x1_start()
    el1[...] = dot3(re1[...], S1[0, 3:19, 8:24, :].reshape(256, 128), True)
    e1[k] = el1[...]
    g1_start, g1_recv, g1_send = gather(2, el1, e1)
    g1_start()
    smoothed(0)

    g1_recv()
    phi = dot3(L1, e1[...].reshape(256, 256))
    S1[1, 3:19, 8:24, :] = phi.T.reshape(16, 16, 128)
    y1_start, y1_recv, y1_send = halo(2, S1, 1, 3, 16, 3)
    y1_start()
    x1_recv()
    y1_recv()
    residual(1)

    def put2(h, i, v):
        S2[h, 3 + i, 8:16, :] = v
    restrict(1, put2)
    x2_start, x2_recv, x2_send = halo(3, S2, None, 3, 8, 3)
    x2_start()
    smoothed(1)

    x2_recv()
    residual(2)

    def put3(h, i, v):
        fb3[h, i, 0:4, :] = v
    restrict(2, put3)
    x3_start, x3_recv, x3_send = whole(4, fb3, rb3)
    x3_start()
    smoothed(2)

    x3_recv()
    unpack(S3, fb3, rb3, 4)
    residual(3)

    def put4(h, i, v):
        fb4[h, i, 0:2, :] = v
    restrict(3, put4)
    x4_start, x4_recv, x4_send = whole(5, fb4, rb4)
    x4_start()
    smoothed(3)

    x4_recv()
    unpack(S4, fb4, rb4, 2)
    ta4 = at("TA", 4)
    solve(4, S4, ta4)

    def putm4(h, x, v):
        mb4[h, x - 4, 0:2, :] = v[4:6]
    stencil(4, ta4, putm4, 0, lambda h, x, v: 0.96 * S4[h, x] + 0.64 * v)
    z4_start, z4_recv, z4_send = whole(6, mb4, qb4)
    z4_start()
    z4_recv()
    unpack(M4, mb4, qb4, 2)

    def putm3(h, x, v):
        mb3[h, x - 4, 0:4, :] = v[4:8]
    correct(3, putm3)
    z3_start, z3_recv, z3_send = whole(7, mb3, qb3)
    z3_start()
    z3_recv()
    unpack(M3, mb3, qb3, 4)

    def putm2(h, x, v):
        M2[h, x, 8:16, :] = v[8:16]
    correct(2, putm2)
    z2_start, z2_recv, z2_send = halo(8, M2, None, 3, 8, 2)
    z2_start()
    z2_recv()

    def putm1(h, x, v):
        M1[h, x, 8:24, :] = v[8:24]
    correct(1, putm1)
    z1_start, z1_recv, z1_send = halo(9, M1, None, 3, 16, 2)
    z1_start()
    z1_recv()

    mo = at("BB", 0)
    correct(0, into(mo))
    tm = at("TB", 0)
    solve(0, mo, tm)
    inv0 = 1.0 / a[0]

    def putout(h, x, v):
        res_ref[x - 4] = v[8:40]
        sol_ref[x - 4] = (inv0 * tm[0, x])[8:40]
    stencil(0, tm, putout, 0, lambda h, x, v: (S0[0, x] - mo[0, x]) + v, (0,))

    for wait in sends + [
        x1_send, g1_send, y1_send, x2_send, x3_send, x4_send, z4_send, z3_send, z2_send, z1_send
    ]:
        wait()


def body(sizes, right_side, z_faces, xy_coupling, block_inverse):
    n = right_side.shape
    vmem = pl.BlockSpec(memory_space=pltpu.VMEM)
    scratch = [pltpu.VMEM(s, f32) for s in scratch_shapes().values()]
    scratch += [pltpu.VMEM((5, 256, 256), bf16), pltpu.VMEM((5, 256, 256), bf16)]
    scratch += [pltpu.SemaphoreType.DMA((10, 8)), pltpu.SemaphoreType.DMA((10, 8))]
    scratch += [pltpu.SemaphoreType.DMA((3, 8)), pltpu.SemaphoreType.DMA((3, 8))]
    return pl.pallas_call(
        lambda *r: kernel(sizes, *r),
        out_shape=(jax.ShapeDtypeStruct(n, f32), jax.ShapeDtypeStruct(n, f32)),
        in_specs=[vmem, vmem, vmem, pl.BlockSpec(memory_space=pltpu.SMEM)],
        out_specs=(vmem, vmem),
        scratch_shapes=scratch,
        compiler_params=pltpu.CompilerParams(
            collective_id=0, has_side_effects=True, vmem_limit_bytes=60 * 2**20
        ),
        name="vcycle",
    )(right_side, z_faces.reshape(1, -1), block_inverse, xy_coupling)


def solution(mesh):
    sizes = tuple(mesh.shape[n] for n in ("gx", "gy", "gz"))
    return jax.shard_map(
        lambda *args: body(sizes, *args),
        mesh=mesh,
        in_specs=(P("gx", "gy", "gz"), P("gz"), P(), P(None, "gz", None)),
        out_specs=(P("gx", "gy", "gz"), P("gx", "gy", "gz")),
        check_vma=False,
    )
```

time: 718 us -> 92.1 us (0.13); the launches traced: 705 us -> 90.5 us
  starting transfers between devices: 370 us -> 0 us
  blocking collectives: 128 us -> 0 us
  waiting for transfers between devices: 108 us -> 0 us
  Pallas kernels: 0 us -> 87.1 us
  other arithmetic: 46.6 us -> 0 us
  local copies, waits for them, and re-layouts: 26.5 us -> 2.72 us
  matrix products: 21.8 us -> 0 us
    ppermute x124 -> x0, starting transfers between devices: 317 us -> none  [the longest x54 164 us: extended(): lax.ppermute(last, axis, up)]
    all_to_all x10 -> x0, blocking collectives: 117 us -> none  [copy_for_each(): lax.all_to_all(jnp.broadcast_to(value[None], (size, *value.shape)), axis,...]
    pallas_call x0 -> x1, Pallas kernels: none -> 87.1 us  [body(): pl.pallas_call(lambda *r: kernel(sizes, *r), out_shape=(jax.ShapeDtypeStr...]
    ppermute x124 -> x0, waiting for transfers between devices: 74.2 us -> none  [the longest x54 46.7 us: extended(): lax.ppermute(initial, axis, [(b, a) for a, b in up])]
    all_to_all x8 -> x0, starting transfers between devices: 52.5 us -> none  [copy_for_each(): lax.all_to_all(jnp.broadcast_to(value[None], (size, *value.shape)), axis,...]
    all_to_all x8 -> x0, waiting for transfers between devices: 34.3 us -> none  [copy_for_each(): lax.all_to_all(jnp.broadcast_to(value[None], (size, *value.shape)), axis,...]
    another operation x71 -> x0, other arithmetic: 20.6 us -> none  [the longest x15 10.7 us: interface_setup(): return (corner_inverse, diagonal_part, jnp.linalg.cholesky(schur_matrix))]
    dot_general x36 -> x0, matrix products: 19.8 us -> none  [the longest x18 17.3 us: solve(): jnp.einsum('xyj,ij->xyi', source, inverse_block, precision=highest)]
  transfers between devices with their start and end apart: 132 -> 0, of which waited for: 40 -> 0; matrix products, arithmetic and copies ran while one was open for 4% -> 0% of each run, Pallas kernels for 0% -> 0%
where the time goes in v1:
time: 92.1 us; the launch traced here: 90.5 us
  Pallas kernels  87.1 us (95%)
  local copies, waits for them, and re-layouts  2.72 us (3%)
    pallas_call x1, Pallas kernels, body(): pl.pallas_call(lambda *r: kernel(sizes, *r), out_shape=(jax.ShapeDtypeStr...  87.1 us
    unnamed x4, local copies, waits for them, and re-layouts  2.72 us

profile of v1, /device:TPU:2, one launch (start us, length us, event | category | flops | bytes accessed | tf_op | source)
XLA Modules:
  0.0 90.5 jit_solution(10235722715194791067)
XLA Ops:
  0.6 87.1 %vcycle.1 = (f32[32,32,128]{2,1,0:T(8,128)}, f32[32,32,128]{2,1,0:T(8,128)}) custom-call(f32[32,32,128]{2,1,0:T(8,128)} %r_0_.1, f32[1,128]{1,0:T(1,128)} %bitcast.1, f32[5,128,128]{2,1,0:T(8,128)} %r_2_.1, f32[5]{0:T(128)} %r_3_.1), custom_call_target="tpu_custom_call" | custom-call | tf_op jit(solution)/shard_map/vcycle/pallas_call | solution.py:628
  87.8 0.0 copy-start
  87.8 1.9 %copy.8 = f32[32,32,128]{2,1,0:T(8,128)} copy(f32[32,32,128]{2,1,0:T(8,128)} %get-tuple-element.4) | data formatting | bytes 1048576
  89.7 0.0 copy-done
  89.7 0.8 copy.9
Async XLA Ops:
  87.8 1.9 %copy-start = (f32[32,32,128]{2,1,0:T(8,128)S(1)}, f32[32,32,128]{2,1,0:T(8,128)}, u32[]{:S(2)}) copy-start(f32[32,32,128]{2,1,0:T(8,128)} %get-tuple-element.5) | copy-start | bytes 1572868

commit v2 on v1

--- a/solution.py
+++ b/solution.py
@@ -54,6 +54,9 @@
 
 def iota(shape, dim):
     return lax.broadcasted_iota(jnp.int32, shape, dim)
+
+
+MESSAGES = {"f1": 2, "s2": 5, "s3": 3, "s4": 1, "m4": 1, "m3": 3, "m2": 5, "m1": 10}
 
 
 def scratch_shapes():
@@ -65,32 +68,33 @@
         if l:
             for t in ("M", "U", "V"):
                 out[f"{t}{l}"] = (2, SX[l], SY[l], 128)
-    out["fb3"] = out["mb3"] = (2, 4, 8, 128)
-    out["fb4"] = out["mb4"] = (2, 2, 8, 128)
-    out["rb3"] = out["qb3"] = (8, 2, 4, 8, 128)
-    out["rb4"] = out["qb4"] = (8, 2, 2, 8, 128)
+    out["C0"] = (4, SX[0], SY[0], 128)
+    out["HM"] = out["H2"] = (2, SX[1], SY[1], 128)
+    for name, tiles in MESSAGES.items():
+        out["out_" + name] = out["in_" + name] = (8, tiles, 8, 128)
     out["rows"] = (4, 16, 128)
     out["re0"] = (8, 128)
     out["re1"] = (32, 128)
     out["cg"] = (9, 16, 128)
     out["cgl"] = (16, 128)
-    out["e0"] = (8, 8, 1920)
+    out["e0"] = (8, 8, 1024)
+    out["eh"] = (8, 8, 640)
     out["e1"] = (8, 32, 256)
-    out["el0"] = (8, 1920)
+    out["el0"] = (8, 1024)
+    out["elh"] = (8, 640)
     out["el1"] = (32, 256)
     return out
 
 
-def kernel(sizes, f_ref, zf_ref, g_ref, e_ref, sol_ref, res_ref, *refs):
+def kernel(sizes, f_ref, zf_ref, ginv_ref, e_ref, sol_ref, res_ref, *refs):
     names = list(scratch_shapes())
     r_ = dict(zip(names, refs))
-    th, tl, hs, hr, gs, gr = refs[len(names):]
+    g_ref, th, tl, ra, ub, hs, hr, gs, gr, ls = refs[len(names):]
     S0, S1, S2, S3, S4 = [r_[f"S{l}"] for l in range(5)]
     M1, M2, M3, M4 = [r_[f"M{l}"] for l in range(1, 5)]
-    fb3, fb4, mb3, mb4 = r_["fb3"], r_["fb4"], r_["mb3"], r_["mb4"]
-    rb3, rb4, qb3, qb4 = r_["rb3"], r_["rb4"], r_["qb3"], r_["qb4"]
     rows, re0, re1, cg, cgl = r_["rows"], r_["re0"], r_["re1"], r_["cg"], r_["cgl"]
     e0, e1, el0, el1 = r_["e0"], r_["e1"], r_["el0"], r_["el1"]
+    eh, elh, C0, HM, H2 = r_["eh"], r_["elh"], r_["C0"], r_["HM"], r_["H2"]
 
     ngx, ngy, ngz = sizes
     ix, iy, k = lax.axis_index("gx"), lax.axis_index("gy"), lax.axis_index("gz")
@@ -121,10 +125,29 @@
             return c
         lax.fori_loop(0, ref.shape[1], step, 0)
 
-    for r in (S0, S1, S2, S3, S4, M1, M2, M3, M4):
-        clear2(r)
-    for r in (cg, e0, e1, rb3, rb4, qb3, qb4, fb3, fb4, mb3, mb4, rows):
-        clear(r)
+    load_f = pltpu.make_async_copy(f_ref, S0.at[0, 4:36, 8:40, :], ls.at[0])
+    load_g = pltpu.make_async_copy(ginv_ref, g_ref, ls.at[1])
+    load_f.start()
+    load_g.start()
+
+    def edge(i, c):
+        S0[0, i] = jnp.zeros((48, 128), f32)
+        S0[0, 36 + i] = jnp.zeros((48, 128), f32)
+        return c
+    lax.fori_loop(0, 4, edge, 0)
+
+    def sides(i, c):
+        S0[0, 4 + i, 0:8, :] = jnp.zeros((8, 128), f32)
+        S0[0, 4 + i, 40:48, :] = jnp.zeros((8, 128), f32)
+        return c
+    lax.fori_loop(0, 32, sides, 0)
+    clear2(S1)
+    clear(r_["in_f1"])
+    clear(rows)
+    if ngz < 8:
+        for r in (e0, eh, e1):
+            clear(r)
+    clear(cg)
 
     barrier = pltpu.get_barrier_semaphore()
     count = jnp.int32(ngz - 1)
@@ -187,10 +210,143 @@
             return buf.at[half, sx, sy, :], buf.at[half, tx, ty, :]
         return exchange(phase, pick)
 
-    def whole(phase, blk, rbuf):
+    def lanes_of(planes):
+        out = planes[0]
+        for i, v in enumerate(planes[1:]):
+            out = out + pltpu.roll(v, 32 * (i + 1), 1)
+        return out
+
+    low_lanes = {r: iota((r, 128), 1) < 32 for r in (8,)}
+
+    def lanes_back(tile, i):
+        v = tile if i == 0 else pltpu.roll(tile, 128 - 32 * i, 1)
+        return jnp.where(low_lanes[8], v, 0.0)
+
+    def tiles_of(l, dx, dy, both):
+        n = LX[l]
+        if dx == 0:
+            return (n // 2 if both else 0) + (n + 7) // 8
+        if dy == 0:
+            return (3 * n // 8 if both else 0) + n // 8
+        return 2 if both else 1
+
+    def packed(phase, l, name, buf, both=True):
+        n, ox, oy = LX[l], OX[l], OY[l]
+        ob, ib = r_["out_" + name], r_["in_" + name]
+
         def pick(dx, dy):
-            return blk, rbuf.at[DIRS.index((dx, dy))]
-        return exchange(phase, pick)
+            d, t = DIRS.index((dx, dy)), tiles_of(l, dx, dy, both)
+            return ob.at[d, 0:t], ib.at[d, 0:t]
+
+        start0, wait_recv, wait_send = exchange(phase, pick)
+
+        def start():
+            for d, (dx, dy) in enumerate(DIRS):
+                xs = ox + n - 3 if dx == 1 else ox
+                ys = oy + n - 4 if dy == 1 else oy
+                yt = oy + n - 8 if dy == 1 else oy
+                part = slice(4, 8) if dy == 1 else slice(0, 4)
+                if dx == 0:
+                    base = n // 2 if both else 0
+                    if both:
+                        for t in range(n // 2):
+                            ob[d, t, 0:4, :] = buf[0, ox + t, ys : ys + 4, :]
+                            ob[d, t, 4:8, :] = buf[0, ox + t + n // 2, ys : ys + 4, :]
+                    for b in range(n // 4):
+                        v = lanes_of([buf[1, ox + 4 * b + i, yt : yt + 8, :] for i in range(4)])
+                        r = 4 * (b % 2)
+                        ob[d, base + b // 2, r : r + 4, :] = v[part]
+                elif dy == 0:
+                    m = n // 8
+                    base = 3 * m if both else 0
+                    for r in range(m):
+                        y = slice(oy + 8 * r, oy + 8 * r + 8)
+                        if both:
+                            for i in range(3):
+                                ob[d, i * m + r] = buf[0, xs + i, y, :]
+                        ob[d, base + r] = lanes_of([buf[1, xs + i, y, :] for i in range(3)])
+                else:
+                    if both:
+                        ob[d, 0, 0:4, :] = buf[0, xs, ys : ys + 4, :]
+                        ob[d, 0, 4:8, :] = buf[0, xs + 1, ys : ys + 4, :]
+                        ob[d, 1, 0:4, :] = buf[0, xs + 2, ys : ys + 4, :]
+                    v = lanes_of([buf[1, xs + i, yt : yt + 8, :] for i in range(3)])
+                    ob[d, 1 if both else 0, 4:8, :] = v[part]
+            start0()
+
+        def finish():
+            wait_recv()
+            for d, (dx, dy) in enumerate(DIRS):
+                xd = ox - 3 if dx == 1 else ox + n
+                yd = oy - 4 if dy == 1 else oy + n
+                if dx == 0:
+                    base = n // 2 if both else 0
+                    if both:
+                        for t in range(n // 2):
+                            buf[0, ox + t, yd : yd + 4, :] = ib[d, t, 0:4, :]
+                            buf[0, ox + t + n // 2, yd : yd + 4, :] = ib[d, t, 4:8, :]
+                    for b in range(n // 4):
+                        tile, r = ib[d, base + b // 2], 4 * (b % 2)
+                        for i in range(4):
+                            v = lanes_back(tile, i)
+                            buf[1, ox + 4 * b + i, yd : yd + 4, :] = v[r : r + 4]
+                elif dy == 0:
+                    m = n // 8
+                    base = 3 * m if both else 0
+                    for r in range(m):
+                        y = slice(oy + 8 * r, oy + 8 * r + 8)
+                        for i in range(3):
+                            if both:
+                                buf[0, xd + i, y, :] = ib[d, i * m + r]
+                            buf[1, xd + i, y, :] = lanes_back(ib[d, base + r], i)
+                else:
+                    if both:
+                        buf[0, xd, yd : yd + 4, :] = ib[d, 0, 0:4, :]
+                        buf[0, xd + 1, yd : yd + 4, :] = ib[d, 0, 4:8, :]
+                        buf[0, xd + 2, yd : yd + 4, :] = ib[d, 1, 0:4, :]
+                    tile = ib[d, 1 if both else 0]
+                    for i in range(3):
+                        buf[1, xd + i, yd : yd + 4, :] = lanes_back(tile, i)[4:8]
+
+        return start, finish, wait_send
+
+    def packed_block(phase, l, name, buf):
+        n = LX[l]
+        ob, ib = r_["out_" + name], r_["in_" + name]
+
+        def pick(dx, dy):
+            return ob.at[0], ib.at[DIRS.index((dx, dy))]
+
+        start0, wait_recv, wait_send = exchange(phase, pick)
+
+        def start():
+            phi = lanes_of([buf[1, 4 + i, 0:8, :] for i in range(n)])
+            if n == 4:
+                for i in range(4):
+                    r = 4 * (i // 2)
+                    ob[0, i % 2, r : r + 4, :] = buf[0, 4 + i, 4:8, :]
+                ob[0, 2] = phi
+            else:
+                ob[0, 0, 0:2, :] = buf[0, 4, 4:6, :]
+                ob[0, 0, 2:4, :] = buf[0, 5, 4:6, :]
+                ob[0, 0, 4:8, :] = phi[4:8]
+            start0()
+
+        def finish():
+            wait_recv()
+            for d, (dx, dy) in enumerate(DIRS):
+                xd, yd = 4 - n * dx, 4 - n * dy
+                tile = ib[d, 2 if n == 4 else 0]
+                for i in range(n):
+                    v = lanes_back(tile, i)
+                    buf[1, xd + i, yd : yd + n, :] = v[4 : 4 + n]
+                    if n == 4:
+                        r = 4 * (i // 2)
+                        buf[0, xd + i, yd : yd + 4, :] = ib[d, i % 2, r : r + 4, :]
+                    else:
+                        buf[0, xd + i, yd : yd + 2, :] = tile[2 * i : 2 * i + 2]
+
+        return start, finish, wait_send
 
     def gather(phase, src, buf):
         def copy(o):
@@ -216,6 +372,17 @@
 
     sends = []
 
+    def pick0(dx, dy):
+        sx, tx = span(dx, 4, 32, 4)
+        sy, ty = span(dy, 8, 32, 8)
+        return S0.at[0, sx, sy, :], S0.at[0, tx, ty, :]
+
+    load_f.wait()
+    pl.semaphore_wait(barrier, count)
+    h_start, h_recv, h_send = exchange(0, pick0)
+    h_start()
+
+    load_g.wait()
     a = [4.0 * e_ref[l] for l in range(5)]
     for l in range(5):
         rows[0, 2 * l : 2 * l + 1, :] = a[l] * g_ref[l, 0:1, :]
@@ -239,36 +406,39 @@
     cgl[...] = tile
     cg[k] = tile
 
-    def put_f(i, c):
-        S0[0, 4 + i, 8:40, :] = f_ref[i]
-        return c
-    lax.fori_loop(0, 32, put_f, 0)
-
-    pl.semaphore_wait(barrier, count)
-
     c_start, c_recv, c_send = gather(0, cgl, cg)
     c_start()
-
-    def pick0(dx, dy):
-        sx, tx = span(dx, 4, 32, 4)
-        sy, ty = span(dy, 8, 32, 8)
-        sx0, _ = span(dx, 0, 32, 4)
-        sy0, _ = span(dy, 0, 32, 8)
-        return f_ref.at[sx0, sy0, :], S0.at[0, tx, ty, :]
-
-    h_start, h_recv, h_send = exchange(0, pick0)
-    h_start()
-    sends += [c_send, h_send]
-
-    h_recv()
     r0 = re0[...]
-    for i in range(5):
-        fx = S0[0, 8 * i : 8 * i + 8].reshape(384, 128)
-        el0[:, 384 * i : 384 * i + 384] = dot3(r0, fx, True)
+    for i in range(4):
+        fx = S0[0, 4 + 8 * i : 12 + 8 * i, 8:40, :].reshape(256, 128)
+        el0[:, 256 * i : 256 * i + 256] = dot3(r0, fx, True)
     e0[k] = el0[...]
     g0_start, g0_recv, g0_send = gather(1, el0, e0)
     g0_start()
-    sends.append(g0_send)
+    for l in range(1, 5):
+        if l > 1:
+            clear2(S[l])
+        clear2(M[l])
+    for name in MESSAGES:
+        if name != "f1":
+            clear(r_["in_" + name])
+
+    def side_phi(i, c):
+        S0[1, 4 + i, 0:8, :] = jnp.zeros((8, 128), f32)
+        S0[1, 4 + i, 40:48, :] = jnp.zeros((8, 128), f32)
+        return c
+    lax.fori_loop(0, 32, side_phi, 0)
+
+    h_recv()
+    elh[:, 0:384] = dot3(
+        r0, jnp.concatenate([S0[0, 0:4].reshape(192, 128), S0[0, 36:40].reshape(192, 128)], 0), True
+    )
+    fx = jnp.concatenate([S0[0, 4:36, 4:8, :], S0[0, 4:36, 40:44, :]], 1).reshape(256, 128)
+    elh[:, 384:640] = dot3(r0, fx, True)
+    eh[k] = elh[...]
+    gh_start, gh_recv, gh_send = gather(3, elh, eh)
+    gh_start()
+    sends += [h_send, c_send, g0_send, gh_send]
 
     c_recv()
     CG = cg[0:8].reshape(128, 128)
@@ -386,6 +556,21 @@
         th[l, 128:256, 128:256] = qh
         tl[l, 128:256, 128:256] = ql
 
+    gt = a[0] * g_ref[0].T
+    gh, gl = split(gt)
+    ra[0:128, 0:128] = gh
+    ra[128:256, 0:128] = gh
+    ra[0:128, 128:256] = gl
+    ra[128:256, 128:256] = jnp.zeros((128, 128), bf16)
+    gt = g_ref[0].T
+    for i in range(4):
+        row = ri & 31
+        u = jnp.where(row == 12 + i, jnp.broadcast_to(cm * gt[0:1], (128, 128)), 0.0)
+        u = jnp.where(row == 28 + i, jnp.broadcast_to(cp * gt[127:128], (128, 128)), u)
+        uh, ul = split(u)
+        u = jnp.where(ri < 64, uh.astype(f32), jnp.where(ri < 96, ul.astype(f32), 0.0))
+        ub[:, 128 * i : 128 * i + 128] = u.astype(bf16)
+
     def apply(l, src, dst, step, n, scale=None):
         y = src.shape[2]
 
@@ -429,7 +614,7 @@
         return put
 
     def solve(l, src, dst, matrix=None, scale=None):
-        step, n = (8, 5) if l == 0 else (SX[l], 1)
+        step, n = SX[l], 1
         apply(l if matrix is None else matrix, src, dst, step, n, scale)
 
     def residual(l, halves=(0, 1)):
@@ -441,7 +626,7 @@
         stencil(l, bb, into(aa), 0, lambda h, x, v: 0.04 * s[h, x] + v, halves)
 
     def smoothed(l):
-        w = 1 if l == 0 else 0
+        w = 0
         s, ta, tb, tc = S[l], at("TA", l), at("TB", l), at("TC", l)
         bb, cc, ma = at("BB", l), at("CC", l), at("MA", l)
         solve(l, tb, tc)
@@ -465,58 +650,95 @@
 
         lax.fori_loop(0, n, body, 0)
 
-    def unpack(dst, blk, rbuf, n):
-        for h in range(2):
-            for i in range(n):
-                dst[h, 4 + i, 4 : 4 + n, :] = blk[h, i, 0:n, :]
-                for d, (dx, dy) in enumerate(DIRS):
-                    dst[h, 4 - n * dx + i, 4 - n * dy : 4 - n * dy + n, :] = rbuf[d, h, i, 0:n, :]
+    def prolong(l, fields, outs, halves):
+        c = l + 1
+        w = 1 if l == 0 else 0
+        n, ox, oc, y = LX[c], OX[l], OX[c], SY[c]
+        ys, cnt = [(4, 24), (4, 16), (0, 12), (2, 8)][l]
+        gyc = iota((cnt, 128), 0) + (iy * n + ys - OY[c])
+        ym = jnp.where((gyc >= 0) & (gyc < ngy * n), 1.0, 0.0).astype(f32)
+
+        def body(j, carry):
+            j = j - (1 + w)
+            gx = ix * n + j
+            s = jnp.where((gx >= 0) & (gx < ngx * n), 1.0, 0.0).astype(f32)
+            ms = ym * s
+            for h in halves:
+                lower, here, upper = (fields(h, oc + j + i) for i in (-1, 0, 1))
+                for (o, oh), lo_, he, up_ in zip(outs, lower, here, upper):
+                    oh = h if oh is None else oh
+                    for i, far in enumerate((lo_, up_)):
+                        v = 0.75 * he + 0.25 * far
+                        ev = (0.75 * v + 0.25 * pltpu.roll(v, 1, 0))[ys : ys + cnt]
+                        od = (0.75 * v + 0.25 * pltpu.roll(v, y - 1, 0))[ys : ys + cnt]
+                        o[oh, ox + 2 * j + i, pl.ds(0, cnt, 2), :] = ms * ev
+                        o[oh, ox + 2 * j + i, pl.ds(1, cnt, 2), :] = ms * od
+            return carry
+
+        lax.fori_loop(0, n + 2 + 2 * w, body, 0)
 
     def correct(l, store):
         c = l + 1
-        w = 1 if l == 0 else 0
         m, u, g2 = M[c], at("U", c), at("V", c)
         kap = a[l] / a[c]
         solve(c, m, u, c, kap)
         solve(c, u, g2, l, 0.64)
         q = 0.04 * (1.0 - a[c] / a[l])
-        n, ox, oc = LX[c], OX[l], OX[c]
-        y = SY[c]
-        ys, cnt = [(4, 24), (4, 16), (0, 12), (2, 8)][l]
-        gyc = iota((cnt, 128), 0) + (iy * n + ys - OY[c])
-        ym = jnp.where((gyc >= 0) & (gyc < ngy * n), 1.0, 0.0).astype(f32)
         outs = [at("P0", l), at("P1", l), at("P2", l)]
 
         def fields(h, x):
             uv = u[h, x]
             return (0.04 * m[h, x] + q * uv, 0.32 * uv, g2[h, x])
 
-        def body(j, carry):
-            j = j - (1 + w)
-            gx = ix * n + j
-            s = jnp.where((gx >= 0) & (gx < ngx * n), 1.0, 0.0).astype(f32)
-            ms = ym * s
-            for h in range(2):
-                lower, here, upper = (fields(h, oc + j + i) for i in (-1, 0, 1))
-                for o, lo_, he, up_ in zip(outs, lower, here, upper):
-                    for i, far in enumerate((lo_, up_)):
-                        v = 0.75 * he + 0.25 * far
-                        ev = (0.75 * v + 0.25 * pltpu.roll(v, 1, 0))[ys : ys + cnt]
-                        od = (0.75 * v + 0.25 * pltpu.roll(v, y - 1, 0))[ys : ys + cnt]
-                        o[h, ox + 2 * j + i, pl.ds(0, cnt, 2), :] = ms * ev
-                        o[h, ox + 2 * j + i, pl.ds(1, cnt, 2), :] = ms * od
-            return carry
-
-        lax.fori_loop(0, n + 2 + 2 * w, body, 0)
+        prolong(l, fields, [(o, None) for o in outs], (0, 1))
         cc, ma = at("CC", l), at("MA", l)
-        stencil(l, outs[2], into(cc), 1 + w, lambda h, x, v: outs[1][h, x] + v)
-        stencil(l, cc, store, w, lambda h, x, v: (ma[h, x] + outs[0][h, x]) + v)
+        stencil(l, outs[2], into(cc), 1, lambda h, x, v: outs[1][h, x] + v)
+        stencil(l, cc, store, 0, lambda h, x, v: (ma[h, x] + outs[0][h, x]) + v)
+
+    def parts(et):
+        phi = dot3(L0, et).T
+        h, lo_ = split(phi)
+        h, lo_ = h.astype(f32), lo_.astype(f32)
+        return h + pltpu.roll(lo_, 32, 1) + pltpu.roll(h, 64, 1)
+
+    def outside(first):
+        def chunk(i, c):
+            x = pl.ds(i * 8, 8)
+            w = S0[1, x].reshape(384, 128).astype(bf16)
+            t = mm(w, ub[:, 128 * first : 128 * first + 256])
+            C0[first, x] = t[:, 0:128].reshape(8, 48, 128)
+            C0[first + 1, x] = t[:, 128:256].reshape(8, 48, 128)
+            return c
+        lax.fori_loop(0, 5, chunk, 0)
+
+    def power(i, src, dst):
+        def chunk(j, c):
+            x = pl.ds(j * 8, 8)
+            vh, vl = split(src[0, x].reshape(384, 128))
+            t = mm(jnp.concatenate([vh, vl], 1), ra[...])
+            dst[0, x] = (t[:, 0:128] + t[:, 128:256]).reshape(8, 48, 128) + C0[i, x]
+            return c
+        lax.fori_loop(0, 5, chunk, 0)
 
     g0_recv()
-    for i in range(5):
-        phi = dot3(L0, e0[:, :, 384 * i : 384 * i + 384].reshape(64, 384))
-        S0[1, 8 * i : 8 * i + 8] = phi.T.reshape(8, 48, 128)
-    residual(0, (0,))
+    for i in range(4):
+        w = parts(e0[:, :, 256 * i : 256 * i + 256].reshape(64, 256))
+        S0[1, 4 + 8 * i : 12 + 8 * i, 8:40, :] = w.reshape(8, 32, 128)
+    gh_recv()
+    w = parts(eh[:, :, 0:384].reshape(64, 384))
+    S0[1, 0:4] = w[0:192].reshape(4, 48, 128)
+    S0[1, 36:40] = w[192:384].reshape(4, 48, 128)
+    w = parts(eh[:, :, 384:640].reshape(64, 256)).reshape(32, 8, 128)
+    S0[1, 4:36, 4:8, :] = w[:, 0:4]
+    S0[1, 4:36, 40:44, :] = w[:, 4:8]
+
+    t1, t2, t3, t4 = at("TA", 0), at("TB", 0), at("TC", 0), at("P0", 0)
+    aa0, bb0, cc0, ma0 = at("AA", 0), at("BB", 0), at("CC", 0), at("MA", 0)
+    outside(0)
+    power(0, S0, t1)
+    power(1, t1, t2)
+    stencil(0, t2, into(bb0), 1, lambda h, x, v: 0.32 * t1[h, x] + 0.64 * v, (0,))
+    stencil(0, bb0, into(aa0), 0, lambda h, x, v: 0.04 * S0[h, x] + v, (0,))
 
     def put1(h, i, v):
         S1[h, 3 + i, 8:24, :] = v
@@ -527,90 +749,117 @@
     e1[k] = el1[...]
     g1_start, g1_recv, g1_send = gather(2, el1, e1)
     g1_start()
-    smoothed(0)
+
+    outside(2)
+    power(2, t2, t3)
+    power(3, t3, t4)
+
+    def both0(h, x, v):
+        bb0[0, x] = 0.8192 * t3[0, x] + 0.4096 * v
+        bb0[1, x] = 0.4096 * (t3[0, x] + v)
+    stencil(0, t4, both0, 3, lambda h, x, v: v, (0,))
+    stencil(0, bb0, into(cc0), 2, lambda h, x, v: (0.1536 if h else 0.9728) * t2[0, x] + v)
+    stencil(0, cc0, into(aa0), 1, lambda h, x, v: (0.0256 if h else 0.9984) * t1[0, x] + v)
+    stencil(0, aa0, into(ma0), 0, lambda h, x, v: 0.0016 * S0[0, x] + v, (1,))
 
     g1_recv()
     phi = dot3(L1, e1[...].reshape(256, 256))
     S1[1, 3:19, 8:24, :] = phi.T.reshape(16, 16, 128)
-    y1_start, y1_recv, y1_send = halo(2, S1, 1, 3, 16, 3)
+    y1_start, y1_finish, y1_send = packed(2, 1, "f1", S1, False)
     y1_start()
     x1_recv()
-    y1_recv()
+    y1_finish()
     residual(1)
 
     def put2(h, i, v):
         S2[h, 3 + i, 8:16, :] = v
     restrict(1, put2)
-    x2_start, x2_recv, x2_send = halo(3, S2, None, 3, 8, 3)
+    x2_start, x2_finish, x2_send = packed(3, 2, "s2", S2)
     x2_start()
     smoothed(1)
 
-    x2_recv()
+    x2_finish()
     residual(2)
 
     def put3(h, i, v):
-        fb3[h, i, 0:4, :] = v
+        S3[h, 4 + i, 4:8, :] = v
     restrict(2, put3)
-    x3_start, x3_recv, x3_send = whole(4, fb3, rb3)
+    x3_start, x3_finish, x3_send = packed_block(4, 3, "s3", S3)
     x3_start()
     smoothed(2)
 
-    x3_recv()
-    unpack(S3, fb3, rb3, 4)
+    x3_finish()
     residual(3)
 
     def put4(h, i, v):
-        fb4[h, i, 0:2, :] = v
+        S4[h, 4 + i, 4:6, :] = v
     restrict(3, put4)
-    x4_start, x4_recv, x4_send = whole(5, fb4, rb4)
+    x4_start, x4_finish, x4_send = packed_block(5, 4, "s4", S4)
     x4_start()
     smoothed(3)
 
-    x4_recv()
-    unpack(S4, fb4, rb4, 2)
+    x4_finish()
     ta4 = at("TA", 4)
     solve(4, S4, ta4)
 
     def putm4(h, x, v):
-        mb4[h, x - 4, 0:2, :] = v[4:6]
+        M4[h, x, 4:6, :] = v[4:6]
     stencil(4, ta4, putm4, 0, lambda h, x, v: 0.96 * S4[h, x] + 0.64 * v)
-    z4_start, z4_recv, z4_send = whole(6, mb4, qb4)
+    z4_start, z4_finish, z4_send = packed_block(6, 4, "m4", M4)
     z4_start()
-    z4_recv()
-    unpack(M4, mb4, qb4, 2)
+    z4_finish()
 
     def putm3(h, x, v):
-        mb3[h, x - 4, 0:4, :] = v[4:8]
+        M3[h, x, 4:8, :] = v[4:8]
     correct(3, putm3)
-    z3_start, z3_recv, z3_send = whole(7, mb3, qb3)
+    z3_start, z3_finish, z3_send = packed_block(7, 3, "m3", M3)
     z3_start()
-    z3_recv()
-    unpack(M3, mb3, qb3, 4)
+    z3_finish()
 
     def putm2(h, x, v):
         M2[h, x, 8:16, :] = v[8:16]
     correct(2, putm2)
-    z2_start, z2_recv, z2_send = halo(8, M2, None, 3, 8, 2)
+    z2_start, z2_finish, z2_send = packed(8, 2, "m2", M2)
     z2_start()
-    z2_recv()
+    z2_finish()
 
     def putm1(h, x, v):
         M1[h, x, 8:24, :] = v[8:24]
     correct(1, putm1)
-    z1_start, z1_recv, z1_send = halo(9, M1, None, 3, 16, 2)
+    z1_start, z1_finish, z1_send = packed(9, 1, "m1", M1)
     z1_start()
-    z1_recv()
-
-    mo = at("BB", 0)
-    correct(0, into(mo))
-    tm = at("TB", 0)
-    solve(0, mo, tm)
+    z1_finish()
+
+    u, g2 = at("U", 1), at("V", 1)
+    kap = a[0] / a[1]
+    solve(1, M1, u, 1, kap)
+    solve(1, u, g2, 0, 0.64)
+    solve(1, M1, HM, 0)
+    solve(1, g2, H2, 0)
+    q = 0.04 * (1.0 - a[1] / a[0])
+
+    def fields0(h, x):
+        uv, gv = u[0, x], g2[0, x]
+        h0 = 0.04 * HM[0, x] + (q / 0.64) * gv
+        return (0.04 * M1[0, x] + q * uv, h0 - 0.32 * uv, 0.5 * gv, H2[0, x], h0)
+
+    P0, P1, P2 = at("P0", 0), at("P1", 0), at("P2", 0)
+    prolong(0, fields0, [(P0, 0), (P0, 1), (P1, 0), (P1, 1), (P2, 0)], (0,))
+
+    def pair(h, x, v):
+        bb0[0, x] = v - P1[0, x]
+        bb0[1, x] = v + P1[0, x]
+    stencil(0, P1, pair, 2, lambda h, x, v: v, (1,))
+    stencil(0, bb0, into(cc0), 1, lambda h, x, v: P0[1, x] + v, (0,))
     inv0 = 1.0 / a[0]
 
-    def putout(h, x, v):
+    def put_sol(h, x, v):
+        sol_ref[x - 4] = v[8:40]
+
+    def put_res(h, x, v):
         res_ref[x - 4] = v[8:40]
-        sol_ref[x - 4] = (inv0 * tm[0, x])[8:40]
-    stencil(0, tm, putout, 0, lambda h, x, v: (S0[0, x] - mo[0, x]) + v, (0,))
+    stencil(0, bb0, put_sol, 0, lambda h, x, v: inv0 * ((aa0[0, x] + P2[0, x]) + v), (1,))
+    stencil(0, cc0, put_res, 0, lambda h, x, v: (ma0[1, x] - P0[0, x]) + v, (0,))
 
     for wait in sends + [
         x1_send, g1_send, y1_send, x2_send, x3_send, x4_send, z4_send, z3_send, z2_send, z1_send
@@ -621,14 +870,18 @@
 def body(sizes, right_side, z_faces, xy_coupling, block_inverse):
     n = right_side.shape
     vmem = pl.BlockSpec(memory_space=pltpu.VMEM)
+    hbm = pl.BlockSpec(memory_space=pl.ANY)
     scratch = [pltpu.VMEM(s, f32) for s in scratch_shapes().values()]
+    scratch += [pltpu.VMEM((5, 128, 128), f32)]
     scratch += [pltpu.VMEM((5, 256, 256), bf16), pltpu.VMEM((5, 256, 256), bf16)]
+    scratch += [pltpu.VMEM((256, 256), bf16), pltpu.VMEM((128, 512), bf16)]
     scratch += [pltpu.SemaphoreType.DMA((10, 8)), pltpu.SemaphoreType.DMA((10, 8))]
-    scratch += [pltpu.SemaphoreType.DMA((3, 8)), pltpu.SemaphoreType.DMA((3, 8))]
+    scratch += [pltpu.SemaphoreType.DMA((4, 8)), pltpu.SemaphoreType.DMA((4, 8))]
+    scratch += [pltpu.SemaphoreType.DMA((2,))]
     return pl.pallas_call(
         lambda *r: kernel(sizes, *r),
-        out_shape=(jax.ShapeDtypeStruct(n, f32), jax.ShapeDtypeStruct(n, f32)),
-        in_specs=[vmem, vmem, vmem, pl.BlockSpec(memory_space=pltpu.SMEM)],
+        out_shape=(pltpu.VMEM(n, f32), pltpu.VMEM(n, f32)),
+        in_specs=[hbm, vmem, hbm, pl.BlockSpec(memory_space=pltpu.SMEM)],
         out_specs=(vmem, vmem),
         scratch_shapes=scratch,
         compiler_params=pltpu.CompilerParams(

time: 92.1 us -> 80.4 us (0.87); the launches traced: 90.5 us -> 80.3 us
  Pallas kernels: 87.1 us -> 78 us
  local copies, waits for them, and re-layouts: 2.72 us -> 1.59 us
    pallas_call x1, Pallas kernels: 87.1 us -> 78 us  [body(): pl.pallas_call(lambda *r: kernel(sizes, *r), out_shape=(pltpu.VMEM(n, f32...]
    unnamed x4 -> x2, local copies, waits for them, and re-layouts: 2.72 us -> 1.59 us
where the time goes in v2:
time: 80.4 us; the launch traced here: 80.3 us
  Pallas kernels  78 us (97%)
  local copies, waits for them, and re-layouts  1.59 us (2%)
    pallas_call x1, Pallas kernels, body(): pl.pallas_call(lambda *r: kernel(sizes, *r), out_shape=(pltpu.VMEM(n, f32...  78 us

profile of v2, /device:TPU:2, one launch (start us, length us, event | category | flops | bytes accessed | tf_op | source)
XLA Modules:
  0.0 80.3 jit_solution(611273613324806471)
XLA Ops:
  0.6 78.0 %vcycle.1 = (f32[32,32,128]{2,1,0:T(8,128)S(1)}, f32[32,32,128]{2,1,0:T(8,128)S(1)}) custom-call(f32[32,32,128]{2,1,0:T(8,128)} %r_0_.1, f32[1,128]{1,0:T(1,128)} %bitcast.1, f32[5,128,128]{2,1,0:T(8,128)} %r_2_.1, f32[5]{0:T(128)} %r_3_.1), custom_call_target="tpu_custom_call" | custom-call | tf_op jit(solution)/shard_map/vcycle/pallas_call | solution.py:881
  78.7 0.8 copy.8
  79.5 0.8 copy.9

commit v3 on v2

--- a/solution.py
+++ b/solution.py
@@ -9,13 +9,14 @@
 bf16 = jnp.bfloat16
 HI = lax.Precision.HIGHEST
 MESH = pl.DeviceIdType.MESH
+FAR = [(dx, dy) for dx in (-2, -1, 0, 1, 2) for dy in (-2, -1, 0, 1, 2) if 0 < abs(dx) + abs(dy) < 4]
 DIRS = [(dx, dy) for dx in (-1, 0, 1) for dy in (-1, 0, 1) if (dx, dy) != (0, 0)]
 
 LX = [32, 16, 8, 4, 2]
 OX = [4, 3, 3, 4, 4]
-OY = [8, 8, 8, 4, 4]
+OY = [8, 4, 4, 4, 4]
 SX = [40, 22, 14, 12, 10]
-SY = [48, 32, 24, 16, 16]
+SY = [48, 24, 16, 16, 16]
 
 
 def pair_of(p):
@@ -56,7 +57,7 @@
     return lax.broadcasted_iota(jnp.int32, shape, dim)
 
 
-MESSAGES = {"f1": 2, "s2": 5, "s3": 3, "s4": 1, "m4": 1, "m3": 3, "m2": 5, "m1": 10}
+MESSAGES = {"f0": 16, "g1": 8, "f1": 2, "s2": 5, "s3": 3, "s4": 1, "m3": 3, "m2": 5, "m1": 10}
 
 
 def scratch_shapes():
@@ -68,15 +69,15 @@
         if l:
             for t in ("M", "U", "V"):
                 out[f"{t}{l}"] = (2, SX[l], SY[l], 128)
-    out["C0"] = (4, SX[0], SY[0], 128)
     out["HM"] = out["H2"] = (2, SX[1], SY[1], 128)
     for name, tiles in MESSAGES.items():
-        out["out_" + name] = out["in_" + name] = (8, tiles, 8, 128)
+        out["out_" + name] = out["in_" + name] = (len(FAR) if name == "s4" else 8, tiles, 8, 128)
     out["rows"] = (4, 16, 128)
     out["re0"] = (8, 128)
     out["re1"] = (32, 128)
     out["cg"] = (9, 16, 128)
-    out["cgl"] = (16, 128)
+    out["cgl"] = out["cgl2"] = (16, 128)
+    out["cg2"] = (8, 16, 128)
     out["e0"] = (8, 8, 1024)
     out["eh"] = (8, 8, 640)
     out["e1"] = (8, 32, 256)
@@ -94,7 +95,8 @@
     M1, M2, M3, M4 = [r_[f"M{l}"] for l in range(1, 5)]
     rows, re0, re1, cg, cgl = r_["rows"], r_["re0"], r_["re1"], r_["cg"], r_["cgl"]
     e0, e1, el0, el1 = r_["e0"], r_["e1"], r_["el0"], r_["el1"]
-    eh, elh, C0, HM, H2 = r_["eh"], r_["elh"], r_["C0"], r_["HM"], r_["H2"]
+    eh, elh, HM, H2 = r_["eh"], r_["elh"], r_["HM"], r_["H2"]
+    cg2, cgl2 = r_["cg2"], r_["cgl2"]
 
     ngx, ngy, ngz = sizes
     ix, iy, k = lax.axis_index("gx"), lax.axis_index("gy"), lax.axis_index("gz")
@@ -141,17 +143,17 @@
         S0[0, 4 + i, 40:48, :] = jnp.zeros((8, 128), f32)
         return c
     lax.fori_loop(0, 32, sides, 0)
-    clear2(S1)
-    clear(r_["in_f1"])
+    for name in ("f0", "g1", "f1"):
+        clear(r_["in_" + name])
     clear(rows)
     if ngz < 8:
-        for r in (e0, eh, e1):
+        for r in (e0, eh, e1, cg2):
             clear(r)
     clear(cg)
 
     barrier = pltpu.get_barrier_semaphore()
     count = jnp.int32(ngz - 1)
-    for dx, dy in DIRS:
+    for dx, dy in FAR:
         ok = exists(dx, dy)
 
         @pl.when(ok)
@@ -166,7 +168,7 @@
             barrier, inc=1, device_id=(ix, iy, peer(o)), device_id_type=MESH
         )
 
-    def exchange(phase, pick):
+    def exchange(phase, pick, dirs=DIRS):
         def copy(d, dx, dy):
             src, dst = pick(dx, dy)
             return pltpu.make_async_remote_copy(
@@ -175,19 +177,19 @@
             )
 
         def start():
-            for d, (dx, dy) in enumerate(DIRS):
+            for d, (dx, dy) in enumerate(dirs):
                 @pl.when(exists(dx, dy))
                 def _():
                     copy(d, dx, dy).start()
 
         def wait_recv():
-            for d, (dx, dy) in enumerate(DIRS):
+            for d, (dx, dy) in enumerate(dirs):
                 @pl.when(exists(-dx, -dy))
                 def _():
                     copy(d, dx, dy).wait_recv()
 
         def wait_send():
-            for d, (dx, dy) in enumerate(DIRS):
+            for d, (dx, dy) in enumerate(dirs):
                 @pl.when(exists(dx, dy))
                 def _():
                     copy(d, dx, dy).wait_send()
@@ -201,15 +203,6 @@
             return pl.ds(off + n - h, h), pl.ds(off - h, h)
         return pl.ds(off, h), pl.ds(off + n, h)
 
-    def halo(phase, buf, half, ox, n, hx):
-        def pick(dx, dy):
-            sx, tx = span(dx, ox, n, hx)
-            sy, ty = span(dy, 8, n, 8)
-            if half is None:
-                return buf.at[:, sx, sy, :], buf.at[:, tx, ty, :]
-            return buf.at[half, sx, sy, :], buf.at[half, tx, ty, :]
-        return exchange(phase, pick)
-
     def lanes_of(planes):
         out = planes[0]
         for i, v in enumerate(planes[1:]):
@@ -222,20 +215,20 @@
         v = tile if i == 0 else pltpu.roll(tile, 128 - 32 * i, 1)
         return jnp.where(low_lanes[8], v, 0.0)
 
-    def tiles_of(l, dx, dy, both):
+    def tiles_of(l, dx, dy, wf, wp):
         n = LX[l]
         if dx == 0:
-            return (n // 2 if both else 0) + (n + 7) // 8
+            return (n // 2 if wf else 0) + ((n + 7) // 8 if wp else 0)
         if dy == 0:
-            return (3 * n // 8 if both else 0) + n // 8
-        return 2 if both else 1
-
-    def packed(phase, l, name, buf, both=True):
+            return (3 * n // 8 if wf else 0) + (n // 8 if wp else 0)
+        return 2 if wf else 1
+
+    def packed(phase, l, name, buf, wf=True, wp=True):
         n, ox, oy = LX[l], OX[l], OY[l]
         ob, ib = r_["out_" + name], r_["in_" + name]
 
         def pick(dx, dy):
-            d, t = DIRS.index((dx, dy)), tiles_of(l, dx, dy, both)
+            d, t = DIRS.index((dx, dy)), tiles_of(l, dx, dy, wf, wp)
             return ob.at[d, 0:t], ib.at[d, 0:t]
 
         start0, wait_recv, wait_send = exchange(phase, pick)
@@ -244,34 +237,37 @@
             for d, (dx, dy) in enumerate(DIRS):
                 xs = ox + n - 3 if dx == 1 else ox
                 ys = oy + n - 4 if dy == 1 else oy
-                yt = oy + n - 8 if dy == 1 else oy
-                part = slice(4, 8) if dy == 1 else slice(0, 4)
+                yt = ys // 8 * 8
+                part = slice(ys - yt, ys - yt + 4)
                 if dx == 0:
-                    base = n // 2 if both else 0
-                    if both:
+                    base = n // 2 if wf else 0
+                    if wf:
                         for t in range(n // 2):
                             ob[d, t, 0:4, :] = buf[0, ox + t, ys : ys + 4, :]
                             ob[d, t, 4:8, :] = buf[0, ox + t + n // 2, ys : ys + 4, :]
-                    for b in range(n // 4):
-                        v = lanes_of([buf[1, ox + 4 * b + i, yt : yt + 8, :] for i in range(4)])
-                        r = 4 * (b % 2)
-                        ob[d, base + b // 2, r : r + 4, :] = v[part]
+                    if wp:
+                        for b in range(n // 4):
+                            v = lanes_of([buf[1, ox + 4 * b + i, yt : yt + 8, :] for i in range(4)])
+                            r = 4 * (b % 2)
+                            ob[d, base + b // 2, r : r + 4, :] = v[part]
                 elif dy == 0:
                     m = n // 8
-                    base = 3 * m if both else 0
+                    base = 3 * m if wf else 0
                     for r in range(m):
                         y = slice(oy + 8 * r, oy + 8 * r + 8)
-                        if both:
+                        if wf:
                             for i in range(3):
                                 ob[d, i * m + r] = buf[0, xs + i, y, :]
-                        ob[d, base + r] = lanes_of([buf[1, xs + i, y, :] for i in range(3)])
+                        if wp:
+                            ob[d, base + r] = lanes_of([buf[1, xs + i, y, :] for i in range(3)])
                 else:
-                    if both:
+                    if wf:
                         ob[d, 0, 0:4, :] = buf[0, xs, ys : ys + 4, :]
                         ob[d, 0, 4:8, :] = buf[0, xs + 1, ys : ys + 4, :]
                         ob[d, 1, 0:4, :] = buf[0, xs + 2, ys : ys + 4, :]
-                    v = lanes_of([buf[1, xs + i, yt : yt + 8, :] for i in range(3)])
-                    ob[d, 1 if both else 0, 4:8, :] = v[part]
+                    if wp:
+                        v = lanes_of([buf[1, xs + i, yt : yt + 8, :] for i in range(3)])
+                        ob[d, 1 if wf else 0, 4:8, :] = v[part]
             start0()
 
         def finish():
@@ -280,44 +276,47 @@
                 xd = ox - 3 if dx == 1 else ox + n
                 yd = oy - 4 if dy == 1 else oy + n
                 if dx == 0:
-                    base = n // 2 if both else 0
-                    if both:
+                    base = n // 2 if wf else 0
+                    if wf:
                         for t in range(n // 2):
                             buf[0, ox + t, yd : yd + 4, :] = ib[d, t, 0:4, :]
                             buf[0, ox + t + n // 2, yd : yd + 4, :] = ib[d, t, 4:8, :]
-                    for b in range(n // 4):
-                        tile, r = ib[d, base + b // 2], 4 * (b % 2)
-                        for i in range(4):
-                            v = lanes_back(tile, i)
-                            buf[1, ox + 4 * b + i, yd : yd + 4, :] = v[r : r + 4]
+                    if wp:
+                        for b in range(n // 4):
+                            tile, r = ib[d, base + b // 2], 4 * (b % 2)
+                            for i in range(4):
+                                v = lanes_back(tile, i)
+                                buf[1, ox + 4 * b + i, yd : yd + 4, :] = v[r : r + 4]
                 elif dy == 0:
                     m = n // 8
-                    base = 3 * m if both else 0
+                    base = 3 * m if wf else 0
                     for r in range(m):
                         y = slice(oy + 8 * r, oy + 8 * r + 8)
                         for i in range(3):
-                            if both:
+                            if wf:
                                 buf[0, xd + i, y, :] = ib[d, i * m + r]
-                            buf[1, xd + i, y, :] = lanes_back(ib[d, base + r], i)
+                            if wp:
+                                buf[1, xd + i, y, :] = lanes_back(ib[d, base + r], i)
                 else:
-                    if both:
+                    if wf:
                         buf[0, xd, yd : yd + 4, :] = ib[d, 0, 0:4, :]
                         buf[0, xd + 1, yd : yd + 4, :] = ib[d, 0, 4:8, :]
                         buf[0, xd + 2, yd : yd + 4, :] = ib[d, 1, 0:4, :]
-                    tile = ib[d, 1 if both else 0]
-                    for i in range(3):
-                        buf[1, xd + i, yd : yd + 4, :] = lanes_back(tile, i)[4:8]
+                    if wp:
+                        tile = ib[d, 1 if wf else 0]
+                        for i in range(3):
+                            buf[1, xd + i, yd : yd + 4, :] = lanes_back(tile, i)[4:8]
 
         return start, finish, wait_send
 
-    def packed_block(phase, l, name, buf):
+    def packed_block(phase, l, name, buf, dirs=DIRS):
         n = LX[l]
         ob, ib = r_["out_" + name], r_["in_" + name]
 
         def pick(dx, dy):
-            return ob.at[0], ib.at[DIRS.index((dx, dy))]
-
-        start0, wait_recv, wait_send = exchange(phase, pick)
+            return ob.at[0], ib.at[dirs.index((dx, dy))]
+
+        start0, wait_recv, wait_send = exchange(phase, pick, dirs)
 
         def start():
             phi = lanes_of([buf[1, 4 + i, 0:8, :] for i in range(n)])
@@ -334,7 +333,7 @@
 
         def finish():
             wait_recv()
-            for d, (dx, dy) in enumerate(DIRS):
+            for d, (dx, dy) in enumerate(dirs):
                 xd, yd = 4 - n * dx, 4 - n * dy
                 tile = ib[d, 2 if n == 4 else 0]
                 for i in range(n):
@@ -371,43 +370,63 @@
         return start, wait_recv, wait_send
 
     sends = []
+    ob0, ib0 = r_["out_f0"], r_["in_f0"]
 
     def pick0(dx, dy):
-        sx, tx = span(dx, 4, 32, 4)
-        sy, ty = span(dy, 8, 32, 8)
-        return S0.at[0, sx, sy, :], S0.at[0, tx, ty, :]
-
+        d = DIRS.index((dx, dy))
+        if dy == 0:
+            sx, tx = span(dx, 4, 32, 4)
+            return S0.at[0, sx, 8:40, :], S0.at[0, tx, 8:40, :]
+        t = 16 if dx == 0 else 2
+        return ob0.at[d, 0:t], ib0.at[d, 0:t]
+
+    def ends0(dx):
+        return 32 if dx == 1 else 4
+
+    a = [4.0 * e_ref[l] for l in range(5)]
+    lane16 = iota((16, 128), 1)
+
+    def corner_tile(first, last, tile):
+        for n in range(first, last):
+            rn = rows[n]
+            tile = jnp.where(lane16 == 2 * n, jnp.broadcast_to(rn[:, 0:1], (16, 128)), tile)
+            tile = jnp.where(lane16 == 2 * n + 1, jnp.broadcast_to(rn[:, 127:128], (16, 128)), tile)
+        return tile
+
+    load_g.wait()
+    for l in range(5):
+        rows[0, 2 * l : 2 * l + 1, :] = a[l] * g_ref[l, 0:1, :]
+        rows[0, 2 * l + 1 : 2 * l + 2, :] = a[l] * g_ref[l, 127:128, :]
+    tile = corner_tile(
+        0, 1, jnp.where(lane16 == 8, jnp.broadcast_to(zf_ref[0:1, 0:1], (16, 128)), 0.0)
+    )
+    cgl[...] = tile
+    cg[k] = tile
     load_f.wait()
+    for d, (dx, dy) in enumerate(DIRS):
+        ys = 36 if dy == 1 else 8
+        if dy != 0 and dx == 0:
+            for t in range(16):
+                ob0[d, t, 0:4, :] = S0[0, 4 + t, ys : ys + 4, :]
+                ob0[d, t, 4:8, :] = S0[0, 20 + t, ys : ys + 4, :]
+        elif dy != 0:
+            for t in range(4):
+                r = 4 * (t % 2)
+                ob0[d, t // 2, r : r + 4, :] = S0[0, ends0(dx) + t, ys : ys + 4, :]
+
     pl.semaphore_wait(barrier, count)
     h_start, h_recv, h_send = exchange(0, pick0)
     h_start()
-
-    load_g.wait()
-    a = [4.0 * e_ref[l] for l in range(5)]
-    for l in range(5):
-        rows[0, 2 * l : 2 * l + 1, :] = a[l] * g_ref[l, 0:1, :]
-        rows[0, 2 * l + 1 : 2 * l + 2, :] = a[l] * g_ref[l, 127:128, :]
-    for m in range(1, 4):
-        prev = rows[m - 1]
-        for l in range(5):
-            nxt = a[l] * hdot(prev, g_ref[l])
-            rows[m, 2 * l : 2 * l + 2, :] = nxt[2 * l : 2 * l + 2]
-    for m in range(4):
-        re0[2 * m : 2 * m + 2, :] = rows[m, 0:2, :]
-    for p in range(16):
-        l, m = pair_of(p)
-        re1[2 * p : 2 * p + 2, :] = rows[m - 1, 2 * l : 2 * l + 2, :]
-    lane16 = iota((16, 128), 1)
-    tile = jnp.where(lane16 == 8, jnp.broadcast_to(zf_ref[0:1, 0:1], (16, 128)), 0.0)
-    for n in range(4):
-        rn = rows[n]
-        tile = jnp.where(lane16 == 2 * n, jnp.broadcast_to(rn[:, 0:1], (16, 128)), tile)
-        tile = jnp.where(lane16 == 2 * n + 1, jnp.broadcast_to(rn[:, 127:128], (16, 128)), tile)
-    cgl[...] = tile
-    cg[k] = tile
-
     c_start, c_recv, c_send = gather(0, cgl, cg)
     c_start()
+
+    for m in range(4):
+        if m > 0:
+            prev = rows[m - 1]
+            for l in range(5):
+                nxt = a[l] * hdot(prev, g_ref[l])
+                rows[m, 2 * l : 2 * l + 2, :] = nxt[2 * l : 2 * l + 2]
+        re0[2 * m : 2 * m + 2, :] = rows[m, 0:2, :]
     r0 = re0[...]
     for i in range(4):
         fx = S0[0, 4 + 8 * i : 12 + 8 * i, 8:40, :].reshape(256, 128)
@@ -415,12 +434,20 @@
     e0[k] = el0[...]
     g0_start, g0_recv, g0_send = gather(1, el0, e0)
     g0_start()
+    tile = corner_tile(1, 4, jnp.zeros((16, 128), f32))
+    cgl2[...] = tile
+    cg2[k] = tile
+    c2_start, c2_recv, c2_send = gather(4, cgl2, cg2)
+    c2_start()
+
+    for p in range(16):
+        l, m = pair_of(p)
+        re1[2 * p : 2 * p + 2, :] = rows[m - 1, 2 * l : 2 * l + 2, :]
     for l in range(1, 5):
-        if l > 1:
-            clear2(S[l])
+        clear2(S[l])
         clear2(M[l])
     for name in MESSAGES:
-        if name != "f1":
+        if name not in ("f0", "g1", "f1"):
             clear(r_["in_" + name])
 
     def side_phi(i, c):
@@ -430,6 +457,16 @@
     lax.fori_loop(0, 32, side_phi, 0)
 
     h_recv()
+    for d, (dx, dy) in enumerate(DIRS):
+        yd = 4 if dy == 1 else 40
+        if dy != 0 and dx == 0:
+            for t in range(16):
+                S0[0, 4 + t, yd : yd + 4, :] = ib0[d, t, 0:4, :]
+                S0[0, 20 + t, yd : yd + 4, :] = ib0[d, t, 4:8, :]
+        elif dy != 0:
+            for t in range(4):
+                r = 4 * (t % 2)
+                S0[0, (0 if dx == 1 else 36) + t, yd : yd + 4, :] = ib0[d, t // 2, r : r + 4, :]
     elh[:, 0:384] = dot3(
         r0, jnp.concatenate([S0[0, 0:4].reshape(192, 128), S0[0, 36:40].reshape(192, 128)], 0), True
     )
@@ -438,17 +475,19 @@
     eh[k] = elh[...]
     gh_start, gh_recv, gh_send = gather(3, elh, eh)
     gh_start()
-    sends += [h_send, c_send, g0_send, gh_send]
+    sends += [h_send, c_send, c2_send, g0_send, gh_send]
 
     c_recv()
     CG = cg[0:8].reshape(128, 128)
+    CG2 = [None]
     ri, ci = iota((128, 128), 0), iota((128, 128), 1)
     same = (ri >> 1) == (ci >> 1)
     odd = (ci & 1) == 1
     eye = jnp.where(ri == ci, 1.0, 0.0).astype(f32)
 
     def col(c):
-        return jnp.broadcast_to(CG[:, c : c + 1], (128, 128))
+        src = CG2[0] if 2 <= c < 8 else CG
+        return jnp.broadcast_to(src[:, c : c + 1], (128, 128))
 
     def corner(n):
         return jnp.where(same, jnp.where(odd, col(2 * n + 1), col(2 * n)), 0.0)
@@ -474,6 +513,8 @@
         diag = jnp.sum(off * link * dcol, 1, keepdims=True)
         R = R + hdot(hdot(R, off + eye * diag), R)
     W = eye + hdot(R, K)
+    c2_recv()
+    CG2[0] = cg2[...].reshape(128, 128)
     B2, B3, B4 = dot3(corner(1), K), dot3(corner(2), K), dot3(corner(3), K)
     V1 = dot3(W, dot3(B2, W))
     V2 = dot3(W, dot3(B3, W) + dot3(B2, V1))
@@ -513,7 +554,6 @@
         return out
 
     L0 = funct(0)
-    L1 = funct(1)
 
     side_in, side_out = ri >> 4, ci >> 4
     pi, po = ri & 15, ci & 15
@@ -525,36 +565,38 @@
         aout = jnp.where(lo == l, a[l], aout)
     cm = jnp.broadcast_to(zf_ref[0:1, 0:1], (1, 128))
     cp = jnp.broadcast_to(cg[k + 1, 0:1, 8:9], (1, 128))
-    for l in range(5):
-        gt = g_ref[l].T
-        p1 = pid(l, 1)
-        ut = jnp.where(ri == p1, jnp.broadcast_to(cm * gt[0:1], (128, 128)), 0.0)
-        ut = jnp.where(ri == 16 + p1, jnp.broadcast_to(cp * gt[127:128], (128, 128)), ut)
-        if l == 0:
-            q = jnp.where(fl & (pi >= 13) & (pi == po + 1), 1.0, 0.0)
-        else:
-            den = jnp.where(lo == l, 1.0, a[l] - aout)
-            amp = a[l] / den
-            nb = -aout / den
-            p2 = nb * nb
-            p3 = p2 * nb
-            dm = mo - mi
-            pw = jnp.where(dm == 0, 1.0, jnp.where(dm == 1, nb, jnp.where(dm == 2, p2, p3)))
-            pm = jnp.where(mo == 1, nb, jnp.where(mo == 2, p2, jnp.where(mo == 3, p3, p2 * p2)))
-            q = jnp.where((li == lo) & (dm >= 0), amp * pw, 0.0)
-            q = q + jnp.where((li == l) & (mi == 1), pm, 0.0)
-            q = jnp.where(lo == l, jnp.where((li == l) & (mi == mo + 1), 1.0, 0.0), q)
-            q = jnp.where(fl, q, 0.0)
-        for r, v in ((0, a[l] * gt), (128, ut)):
-            vh, vl = split(v)
-            th[l, r : r + 128, 0:128] = vh
-            tl[l, r : r + 128, 0:128] = vl
-        qh, ql = split(q.astype(f32))
-        zero = jnp.zeros((128, 128), bf16)
-        th[l, 0:128, 128:256] = zero
-        tl[l, 0:128, 128:256] = zero
-        th[l, 128:256, 128:256] = qh
-        tl[l, 128:256, 128:256] = ql
+
+    def matrices():
+        for l in range(5):
+            gt = g_ref[l].T
+            p1 = pid(l, 1)
+            ut = jnp.where(ri == p1, jnp.broadcast_to(cm * gt[0:1], (128, 128)), 0.0)
+            ut = jnp.where(ri == 16 + p1, jnp.broadcast_to(cp * gt[127:128], (128, 128)), ut)
+            if l == 0:
+                q = jnp.where(fl & (pi >= 13) & (pi == po + 1), 1.0, 0.0)
+            else:
+                den = jnp.where(lo == l, 1.0, a[l] - aout)
+                amp = a[l] / den
+                nb = -aout / den
+                p2 = nb * nb
+                p3 = p2 * nb
+                dm = mo - mi
+                pw = jnp.where(dm == 0, 1.0, jnp.where(dm == 1, nb, jnp.where(dm == 2, p2, p3)))
+                pm = jnp.where(mo == 1, nb, jnp.where(mo == 2, p2, jnp.where(mo == 3, p3, p2 * p2)))
+                q = jnp.where((li == lo) & (dm >= 0), amp * pw, 0.0)
+                q = q + jnp.where((li == l) & (mi == 1), pm, 0.0)
+                q = jnp.where(lo == l, jnp.where((li == l) & (mi == mo + 1), 1.0, 0.0), q)
+                q = jnp.where(fl, q, 0.0)
+            for r, v in ((0, a[l] * gt), (128, ut)):
+                vh, vl = split(v)
+                th[l, r : r + 128, 0:128] = vh
+                tl[l, r : r + 128, 0:128] = vl
+            qh, ql = split(q.astype(f32))
+            zero = jnp.zeros((128, 128), bf16)
+            th[l, 0:128, 128:256] = zero
+            tl[l, 0:128, 128:256] = zero
+            th[l, 128:256, 128:256] = qh
+            tl[l, 128:256, 128:256] = ql
 
     gt = a[0] * g_ref[0].T
     gh, gl = split(gt)
@@ -589,6 +631,14 @@
 
         lax.fori_loop(0, n, body, 0)
 
+    def solve_block(src, dst):
+        n, y = src.shape[1], src.shape[2]
+        v = jnp.concatenate([src[0].reshape(n * y, 128), src[1].reshape(n * y, 128)], 1)
+        vh, vl = split(v)
+        t = mm(vh, jnp.concatenate([th[0, :, 0:128], tl[0, :, 0:128]], 1))
+        t = t[:, 0:128] + (t[:, 128:256] + mm(vl, th[0, :, 0:128]))
+        dst[0] = t.reshape(n, y, 128)
+
     def stencil(l, src, dst, grow, post, halves=(0, 1)):
         ox, oy, n, y = OX[l], OY[l], LX[l], SY[l]
         gy0 = iota((y, 128), 0) + (iy * n - oy)
@@ -654,7 +704,7 @@
         c = l + 1
         w = 1 if l == 0 else 0
         n, ox, oc, y = LX[c], OX[l], OX[c], SY[c]
-        ys, cnt = [(4, 24), (4, 16), (0, 12), (2, 8)][l]
+        ys, cnt = [(0, 24), (2, 12), (2, 8), (2, 8)][l]
         gyc = iota((cnt, 128), 0) + (iy * n + ys - OY[c])
         ym = jnp.where((gyc >= 0) & (gyc < ngy * n), 1.0, 0.0).astype(f32)
 
@@ -701,24 +751,19 @@
         h, lo_ = h.astype(f32), lo_.astype(f32)
         return h + pltpu.roll(lo_, 32, 1) + pltpu.roll(h, 64, 1)
 
-    def outside(first):
-        def chunk(i, c):
-            x = pl.ds(i * 8, 8)
+    def powers(first, src, d1, d2):
+        for i in range(5):
+            x = slice(8 * i, 8 * i + 8)
             w = S0[1, x].reshape(384, 128).astype(bf16)
-            t = mm(w, ub[:, 128 * first : 128 * first + 256])
-            C0[first, x] = t[:, 0:128].reshape(8, 48, 128)
-            C0[first + 1, x] = t[:, 128:256].reshape(8, 48, 128)
-            return c
-        lax.fori_loop(0, 5, chunk, 0)
-
-    def power(i, src, dst):
-        def chunk(j, c):
-            x = pl.ds(j * 8, 8)
+            c = mm(w, ub[:, 128 * first : 128 * first + 256])
             vh, vl = split(src[0, x].reshape(384, 128))
             t = mm(jnp.concatenate([vh, vl], 1), ra[...])
-            dst[0, x] = (t[:, 0:128] + t[:, 128:256]).reshape(8, 48, 128) + C0[i, x]
-            return c
-        lax.fori_loop(0, 5, chunk, 0)
+            t = (t[:, 0:128] + t[:, 128:256]) + c[:, 0:128]
+            d1[0, x] = t.reshape(8, 48, 128)
+            vh, vl = split(t)
+            t = mm(jnp.concatenate([vh, vl], 1), ra[...])
+            t = (t[:, 0:128] + t[:, 128:256]) + c[:, 128:256]
+            d2[0, x] = t.reshape(8, 48, 128)
 
     g0_recv()
     for i in range(4):
@@ -734,49 +779,46 @@
 
     t1, t2, t3, t4 = at("TA", 0), at("TB", 0), at("TC", 0), at("P0", 0)
     aa0, bb0, cc0, ma0 = at("AA", 0), at("BB", 0), at("CC", 0), at("MA", 0)
-    outside(0)
-    power(0, S0, t1)
-    power(1, t1, t2)
+    powers(0, S0, t1, t2)
     stencil(0, t2, into(bb0), 1, lambda h, x, v: 0.32 * t1[h, x] + 0.64 * v, (0,))
     stencil(0, bb0, into(aa0), 0, lambda h, x, v: 0.04 * S0[h, x] + v, (0,))
 
     def put1(h, i, v):
-        S1[h, 3 + i, 8:24, :] = v
+        S1[h, 3 + i, 4:20, :] = v
     restrict(0, put1, (0,))
-    x1_start, x1_recv, x1_send = halo(1, S1, 0, 3, 16, 3)
-    x1_start()
-    el1[...] = dot3(re1[...], S1[0, 3:19, 8:24, :].reshape(256, 128), True)
+    el1[...] = dot3(re1[...], S1[0, 3:19, 4:20, :].reshape(256, 128), True)
     e1[k] = el1[...]
     g1_start, g1_recv, g1_send = gather(2, el1, e1)
     g1_start()
-
-    outside(2)
-    power(2, t2, t3)
-    power(3, t3, t4)
+    x1_start, x1_finish, x1_send = packed(1, 1, "g1", S1, True, False)
+    x1_start()
+
+    L1 = funct(1)
+    matrices()
+    powers(2, t2, t3, t4)
 
     def both0(h, x, v):
         bb0[0, x] = 0.8192 * t3[0, x] + 0.4096 * v
         bb0[1, x] = 0.4096 * (t3[0, x] + v)
+
+    g1_recv()
+    phi = dot3(L1, e1[...].reshape(256, 256))
+    S1[1, 3:19, 4:20, :] = phi.T.reshape(16, 16, 128)
+    y1_start, y1_finish, y1_send = packed(2, 1, "f1", S1, False, True)
+    y1_start()
     stencil(0, t4, both0, 3, lambda h, x, v: v, (0,))
     stencil(0, bb0, into(cc0), 2, lambda h, x, v: (0.1536 if h else 0.9728) * t2[0, x] + v)
-    stencil(0, cc0, into(aa0), 1, lambda h, x, v: (0.0256 if h else 0.9984) * t1[0, x] + v)
-    stencil(0, aa0, into(ma0), 0, lambda h, x, v: 0.0016 * S0[0, x] + v, (1,))
-
-    g1_recv()
-    phi = dot3(L1, e1[...].reshape(256, 256))
-    S1[1, 3:19, 8:24, :] = phi.T.reshape(16, 16, 128)
-    y1_start, y1_finish, y1_send = packed(2, 1, "f1", S1, False)
-    y1_start()
-    x1_recv()
+    x1_finish()
     y1_finish()
     residual(1)
 
     def put2(h, i, v):
-        S2[h, 3 + i, 8:16, :] = v
+        S2[h, 3 + i, 4:12, :] = v
     restrict(1, put2)
     x2_start, x2_finish, x2_send = packed(3, 2, "s2", S2)
     x2_start()
     smoothed(1)
+    stencil(0, cc0, into(aa0), 1, lambda h, x, v: (0.0256 if h else 0.9984) * t1[0, x] + v)
 
     x2_finish()
     residual(2)
@@ -787,6 +829,7 @@
     x3_start, x3_finish, x3_send = packed_block(4, 3, "s3", S3)
     x3_start()
     smoothed(2)
+    stencil(0, aa0, into(ma0), 0, lambda h, x, v: 0.0016 * S0[0, x] + v, (1,))
 
     x3_finish()
     residual(3)
@@ -794,7 +837,7 @@
     def put4(h, i, v):
         S4[h, 4 + i, 4:6, :] = v
     restrict(3, put4)
-    x4_start, x4_finish, x4_send = packed_block(5, 4, "s4", S4)
+    x4_start, x4_finish, x4_send = packed_block(5, 4, "s4", S4, FAR)
     x4_start()
     smoothed(3)
 
@@ -802,12 +845,7 @@
     ta4 = at("TA", 4)
     solve(4, S4, ta4)
 
-    def putm4(h, x, v):
-        M4[h, x, 4:6, :] = v[4:6]
-    stencil(4, ta4, putm4, 0, lambda h, x, v: 0.96 * S4[h, x] + 0.64 * v)
-    z4_start, z4_finish, z4_send = packed_block(6, 4, "m4", M4)
-    z4_start()
-    z4_finish()
+    stencil(4, ta4, into(M4), 2, lambda h, x, v: 0.96 * S4[h, x] + 0.64 * v)
 
     def putm3(h, x, v):
         M3[h, x, 4:8, :] = v[4:8]
@@ -817,14 +855,14 @@
     z3_finish()
 
     def putm2(h, x, v):
-        M2[h, x, 8:16, :] = v[8:16]
+        M2[h, x, 4:12, :] = v[4:12]
     correct(2, putm2)
     z2_start, z2_finish, z2_send = packed(8, 2, "m2", M2)
     z2_start()
     z2_finish()
 
     def putm1(h, x, v):
-        M1[h, x, 8:24, :] = v[8:24]
+        M1[h, x, 4:20, :] = v[4:20]
     correct(1, putm1)
     z1_start, z1_finish, z1_send = packed(9, 1, "m1", M1)
     z1_start()
@@ -834,8 +872,8 @@
     kap = a[0] / a[1]
     solve(1, M1, u, 1, kap)
     solve(1, u, g2, 0, 0.64)
-    solve(1, M1, HM, 0)
-    solve(1, g2, H2, 0)
+    solve_block(M1, HM)
+    solve_block(g2, H2)
     q = 0.04 * (1.0 - a[1] / a[0])
 
     def fields0(h, x):
@@ -862,7 +900,7 @@
     stencil(0, cc0, put_res, 0, lambda h, x, v: (ma0[1, x] - P0[0, x]) + v, (0,))
 
     for wait in sends + [
-        x1_send, g1_send, y1_send, x2_send, x3_send, x4_send, z4_send, z3_send, z2_send, z1_send
+        x1_send, g1_send, y1_send, x2_send, x3_send, x4_send, z3_send, z2_send, z1_send
     ]:
         wait()
 
@@ -875,8 +913,8 @@
     scratch += [pltpu.VMEM((5, 128, 128), f32)]
     scratch += [pltpu.VMEM((5, 256, 256), bf16), pltpu.VMEM((5, 256, 256), bf16)]
     scratch += [pltpu.VMEM((256, 256), bf16), pltpu.VMEM((128, 512), bf16)]
-    scratch += [pltpu.SemaphoreType.DMA((10, 8)), pltpu.SemaphoreType.DMA((10, 8))]
-    scratch += [pltpu.SemaphoreType.DMA((4, 8)), pltpu.SemaphoreType.DMA((4, 8))]
+    scratch += [pltpu.SemaphoreType.DMA((10, 20)), pltpu.SemaphoreType.DMA((10, 20))]
+    scratch += [pltpu.SemaphoreType.DMA((5, 8)), pltpu.SemaphoreType.DMA((5, 8))]
     scratch += [pltpu.SemaphoreType.DMA((2,))]
     return pl.pallas_call(
         lambda *r: kernel(sizes, *r),

time: 80.4 us -> 75.3 us (0.937)
  Pallas kernels: 78 us -> 72.9 us
    pallas_call x1, Pallas kernels: 78 us -> 72.9 us  [body(): pl.pallas_call(lambda *r: kernel(sizes, *r), out_shape=(pltpu.VMEM(n, f32...]
where the time goes in v3:
time: 75.3 us; the launch traced here: 75.2 us
  Pallas kernels  72.9 us (97%)
  local copies, waits for them, and re-layouts  1.59 us (2%)
    pallas_call x1, Pallas kernels, body(): pl.pallas_call(lambda *r: kernel(sizes, *r), out_shape=(pltpu.VMEM(n, f32...  72.9 us
    unnamed x2, local copies, waits for them, and re-layouts  1.59 us

profile of v3, /device:TPU:2, one launch (start us, length us, event | category | flops | bytes accessed | tf_op | source)
XLA Modules:
  0.0 75.2 jit_solution(10980627509252664798)
XLA Ops:
  0.6 72.9 %vcycle.1 = (f32[32,32,128]{2,1,0:T(8,128)S(1)}, f32[32,32,128]{2,1,0:T(8,128)S(1)}) custom-call(f32[32,32,128]{2,1,0:T(8,128)} %r_0_.1, f32[1,128]{1,0:T(1,128)} %bitcast.1, f32[5,128,128]{2,1,0:T(8,128)} %r_2_.1, f32[5]{0:T(128)} %r_3_.1), custom_call_target="tpu_custom_call" | custom-call | tf_op jit(solution)/shard_map/vcycle/pallas_call | solution.py:919
  73.6 0.8 %copy.8 = f32[32,32,128]{2,1,0:T(8,128)} copy(f32[32,32,128]{2,1,0:T(8,128)S(1)} %get-tuple-element.2) | data formatting | bytes 1048576
  74.4 0.8 %copy.9 = f32[32,32,128]{2,1,0:T(8,128)} copy(f32[32,32,128]{2,1,0:T(8,128)S(1)} %get-tuple-element.3) | data formatting | bytes 1048576

commit v4 on v3

--- a/solution.py
+++ b/solution.py
@@ -87,10 +87,10 @@
     return out
 
 
-def kernel(sizes, f_ref, zf_ref, ginv_ref, e_ref, sol_ref, res_ref, *refs):
+def kernel(sizes, f_ref, zf_in, ginv_ref, e_in, sol_ref, res_ref, *refs):
     names = list(scratch_shapes())
     r_ = dict(zip(names, refs))
-    g_ref, th, tl, ra, ub, hs, hr, gs, gr, ls = refs[len(names):]
+    g_ref, th, tl, ra, ub, hs, hr, gs, gr, ls, zf_ref, e_ref = refs[len(names):]
     S0, S1, S2, S3, S4 = [r_[f"S{l}"] for l in range(5)]
     M1, M2, M3, M4 = [r_[f"M{l}"] for l in range(1, 5)]
     rows, re0, re1, cg, cgl = r_["rows"], r_["re0"], r_["re1"], r_["cg"], r_["cgl"]
@@ -129,27 +129,10 @@
 
     load_f = pltpu.make_async_copy(f_ref, S0.at[0, 4:36, 8:40, :], ls.at[0])
     load_g = pltpu.make_async_copy(ginv_ref, g_ref, ls.at[1])
-    load_f.start()
-    load_g.start()
-
-    def edge(i, c):
-        S0[0, i] = jnp.zeros((48, 128), f32)
-        S0[0, 36 + i] = jnp.zeros((48, 128), f32)
-        return c
-    lax.fori_loop(0, 4, edge, 0)
-
-    def sides(i, c):
-        S0[0, 4 + i, 0:8, :] = jnp.zeros((8, 128), f32)
-        S0[0, 4 + i, 40:48, :] = jnp.zeros((8, 128), f32)
-        return c
-    lax.fori_loop(0, 32, sides, 0)
-    for name in ("f0", "g1", "f1"):
-        clear(r_["in_" + name])
-    clear(rows)
-    if ngz < 8:
-        for r in (e0, eh, e1, cg2):
-            clear(r)
-    clear(cg)
+    load_z = pltpu.make_async_copy(zf_in, zf_ref, ls.at[2])
+    load_e = pltpu.make_async_copy(e_in, e_ref, ls.at[3])
+    for load in (load_e, load_z, load_g, load_f):
+        load.start()
 
     barrier = pltpu.get_barrier_semaphore()
     count = jnp.int32(ngz - 1)
@@ -167,6 +150,28 @@
         pl.semaphore_signal(
             barrier, inc=1, device_id=(ix, iy, peer(o)), device_id_type=MESH
         )
+
+    for d, (dx, dy) in enumerate(DIRS):
+        @pl.when(jnp.logical_not(exists(-dx, -dy)))
+        def _():
+            for name in ("f0", "g1", "f1"):
+                r = r_["in_" + name]
+                for t in range(MESSAGES[name]):
+                    r[d, t] = jnp.zeros((8, 128), f32)
+            if dy == 0:
+                for i in range(4):
+                    S0[0, (0 if dx == 1 else 36) + i, 8:40, :] = jnp.zeros((32, 128), f32)
+
+    def sides(i, c):
+        S0[0, i, 0:8, :] = jnp.zeros((8, 128), f32)
+        S0[0, i, 40:48, :] = jnp.zeros((8, 128), f32)
+        return c
+    lax.fori_loop(0, 40, sides, 0)
+    clear(rows)
+    if ngz < 8:
+        for r in (e0, eh, e1, cg2):
+            clear(r)
+    cg[8] = jnp.zeros((16, 128), f32)
 
     def exchange(phase, pick, dirs=DIRS):
         def copy(d, dx, dy):
@@ -383,6 +388,7 @@
     def ends0(dx):
         return 32 if dx == 1 else 4
 
+    load_e.wait()
     a = [4.0 * e_ref[l] for l in range(5)]
     lane16 = iota((16, 128), 1)
 
@@ -393,6 +399,7 @@
             tile = jnp.where(lane16 == 2 * n + 1, jnp.broadcast_to(rn[:, 127:128], (16, 128)), tile)
         return tile
 
+    load_z.wait()
     load_g.wait()
     for l in range(5):
         rows[0, 2 * l : 2 * l + 1, :] = a[l] * g_ref[l, 0:1, :]
@@ -427,6 +434,12 @@
                 nxt = a[l] * hdot(prev, g_ref[l])
                 rows[m, 2 * l : 2 * l + 2, :] = nxt[2 * l : 2 * l + 2]
         re0[2 * m : 2 * m + 2, :] = rows[m, 0:2, :]
+    tile = corner_tile(1, 4, jnp.zeros((16, 128), f32))
+    cgl2[...] = tile
+    cg2[k] = tile
+    c2_start, c2_recv, c2_send = gather(4, cgl2, cg2)
+    c2_start()
+
     r0 = re0[...]
     for i in range(4):
         fx = S0[0, 4 + 8 * i : 12 + 8 * i, 8:40, :].reshape(256, 128)
@@ -434,12 +447,6 @@
     e0[k] = el0[...]
     g0_start, g0_recv, g0_send = gather(1, el0, e0)
     g0_start()
-    tile = corner_tile(1, 4, jnp.zeros((16, 128), f32))
-    cgl2[...] = tile
-    cg2[k] = tile
-    c2_start, c2_recv, c2_send = gather(4, cgl2, cg2)
-    c2_start()
-
     for p in range(16):
         l, m = pair_of(p)
         re1[2 * p : 2 * p + 2, :] = rows[m - 1, 2 * l : 2 * l + 2, :]
@@ -639,24 +646,53 @@
         t = t[:, 0:128] + (t[:, 128:256] + mm(vl, th[0, :, 0:128]))
         dst[0] = t.reshape(n, y, 128)
 
+    def solves(src, dsts):
+        n, y = src.shape[1], src.shape[2]
+        v = jnp.concatenate([src[0].reshape(n * y, 128), src[1].reshape(n * y, 128)], 1)
+        vh, vl = split(v)
+        for dst, i, scale in dsts:
+            t = mm(vh, th[i]) + (mm(vh, tl[i]) + mm(vl, th[i]))
+            if scale is not None:
+                t = scale * t
+            dst[0] = t[:, 0:128].reshape(n, y, 128)
+            dst[1] = t[:, 128:256].reshape(n, y, 128)
+
+    def product(i, l1, l2):
+        t = mm(th[l1], th[l2]) + (mm(th[l1], tl[l2]) + mm(tl[l1], th[l2]))
+        h, lo_ = split(t)
+        th[i] = h
+        tl[i] = lo_
+
+    def square(l):
+        product(4 + l, l, l)
+
+    def both(l):
+        product(8 + l, l + 1, l)
+
     def stencil(l, src, dst, grow, post, halves=(0, 1)):
         ox, oy, n, y = OX[l], OY[l], LX[l], SY[l]
         gy0 = iota((y, 128), 0) + (iy * n - oy)
         ym = jnp.where((gy0 >= 0) & (gy0 < ngy * n), 0.25, 0.0).astype(f32)
-
-        def body(x, c):
-            gx0 = ix * n + x - ox
-            s = jnp.where((gx0 >= 0) & (gx0 < ngx * n), 1.0, 0.0).astype(f32)
-            m4 = ym * s
+        total = n + 2 * grow
+        step = next(u for u in (4, 3, 2, 1) if total % u == 0)
+
+        def body(i, c):
+            x0 = ox - grow + i * step
+            outs = []
             for h in halves:
-                v = src[h, x]
-                t = (src[h, x - 1] + src[h, x + 1]) + (
-                    pltpu.roll(v, 1, 0) + pltpu.roll(v, y - 1, 0)
-                )
-                dst(h, x, post(h, x, m4 * t))
+                r = [src[h, x0 - 1 + j] for j in range(step + 2)]
+                for j in range(step):
+                    gx0 = ix * n + (x0 + j - ox)
+                    s = jnp.where((gx0 >= 0) & (gx0 < ngx * n), 1.0, 0.0).astype(f32)
+                    t = (r[j] + r[j + 2]) + (
+                        pltpu.roll(r[j + 1], 1, 0) + pltpu.roll(r[j + 1], y - 1, 0)
+                    )
+                    outs.append((h, x0 + j, post(h, x0 + j, (ym * s) * t)))
+            for o in outs:
+                dst(*o)
             return c
 
-        lax.fori_loop(ox - grow, ox + n + grow, body, 0)
+        lax.fori_loop(0, total // step, body, 0)
 
     def into(ref):
         def put(h, x, v):
@@ -670,8 +706,7 @@
     def residual(l, halves=(0, 1)):
         s, ta, tb = S[l], at("TA", l), at("TB", l)
         aa, bb = at("AA", l), at("BB", l)
-        solve(l, s, ta)
-        solve(l, ta, tb)
+        solves(s, [(ta, l, None), (tb, 4 + l, None)])
         stencil(l, tb, into(bb), 1, lambda h, x, v: 0.32 * ta[h, x] + 0.64 * v, halves)
         stencil(l, bb, into(aa), 0, lambda h, x, v: 0.04 * s[h, x] + v, halves)
 
@@ -731,8 +766,7 @@
         c = l + 1
         m, u, g2 = M[c], at("U", c), at("V", c)
         kap = a[l] / a[c]
-        solve(c, m, u, c, kap)
-        solve(c, u, g2, l, 0.64)
+        solves(m, [(u, c, kap), (g2, 8 + l, 0.64 * kap)])
         q = 0.04 * (1.0 - a[c] / a[l])
         outs = [at("P0", l), at("P1", l), at("P2", l)]
 
@@ -796,6 +830,8 @@
     L1 = funct(1)
     matrices()
     powers(2, t2, t3, t4)
+    for l in (1, 2, 3):
+        square(l)
 
     def both0(h, x, v):
         bb0[0, x] = 0.8192 * t3[0, x] + 0.4096 * v
@@ -840,6 +876,8 @@
     x4_start, x4_finish, x4_send = packed_block(5, 4, "s4", S4, FAR)
     x4_start()
     smoothed(3)
+    for l in (3, 2, 1, 0):
+        both(l)
 
     x4_finish()
     ta4 = at("TA", 4)
@@ -870,8 +908,7 @@
 
     u, g2 = at("U", 1), at("V", 1)
     kap = a[0] / a[1]
-    solve(1, M1, u, 1, kap)
-    solve(1, u, g2, 0, 0.64)
+    solves(M1, [(u, 1, kap), (g2, 8, 0.64 * kap)])
     solve_block(M1, HM)
     solve_block(g2, H2)
     q = 0.04 * (1.0 - a[1] / a[0])
@@ -911,15 +948,15 @@
     hbm = pl.BlockSpec(memory_space=pl.ANY)
     scratch = [pltpu.VMEM(s, f32) for s in scratch_shapes().values()]
     scratch += [pltpu.VMEM((5, 128, 128), f32)]
-    scratch += [pltpu.VMEM((5, 256, 256), bf16), pltpu.VMEM((5, 256, 256), bf16)]
+    scratch += [pltpu.VMEM((12, 256, 256), bf16), pltpu.VMEM((12, 256, 256), bf16)]
     scratch += [pltpu.VMEM((256, 256), bf16), pltpu.VMEM((128, 512), bf16)]
     scratch += [pltpu.SemaphoreType.DMA((10, 20)), pltpu.SemaphoreType.DMA((10, 20))]
     scratch += [pltpu.SemaphoreType.DMA((5, 8)), pltpu.SemaphoreType.DMA((5, 8))]
-    scratch += [pltpu.SemaphoreType.DMA((2,))]
+    scratch += [pltpu.SemaphoreType.DMA((4,)), pltpu.VMEM((1, 128), f32), pltpu.SMEM((5,), f32)]
     return pl.pallas_call(
         lambda *r: kernel(sizes, *r),
         out_shape=(pltpu.VMEM(n, f32), pltpu.VMEM(n, f32)),
-        in_specs=[hbm, vmem, hbm, pl.BlockSpec(memory_space=pltpu.SMEM)],
+        in_specs=[hbm, hbm, hbm, hbm],
         out_specs=(vmem, vmem),
         scratch_shapes=scratch,
         compiler_params=pltpu.CompilerParams(

time: 75.3 us -> 69.4 us (0.922)
  Pallas kernels: 72.9 us -> 67.1 us
    pallas_call x1, Pallas kernels: 72.9 us -> 67.1 us  [body(): pl.pallas_call(lambda *r: kernel(sizes, *r), out_shape=(pltpu.VMEM(n, f32...]
where the time goes in v4:
time: 69.4 us; the launch traced here: 69.3 us
  Pallas kernels  67.1 us (97%)
  local copies, waits for them, and re-layouts  1.59 us (2%)
    pallas_call x1, Pallas kernels, body(): pl.pallas_call(lambda *r: kernel(sizes, *r), out_shape=(pltpu.VMEM(n, f32...  67.1 us
    unnamed x2, local copies, waits for them, and re-layouts  1.59 us

profile of v4, /device:TPU:2, one launch (start us, length us, event | category | flops | bytes accessed | tf_op | source)
XLA Modules:
  0.0 69.3 jit_solution(14511062177217615061)
XLA Ops:
  0.6 67.1 %vcycle.1 = (f32[32,32,128]{2,1,0:T(8,128)S(1)}, f32[32,32,128]{2,1,0:T(8,128)S(1)}) custom-call(f32[32,32,128]{2,1,0:T(8,128)} %r_0_.1, f32[1,128]{1,0:T(1,128)} %bitcast.1, f32[5,128,128]{2,1,0:T(8,128)} %r_2_.1, f32[5]{0:T(128)} %r_3_.1), custom_call_target="tpu_custom_call" | custom-call | tf_op jit(solution)/shard_map/vcycle/pallas_call | solution.py:956
  67.7 0.8 %copy.8 = f32[32,32,128]{2,1,0:T(8,128)} copy(f32[32,32,128]{2,1,0:T(8,128)S(1)} %get-tuple-element.2) | data formatting | bytes 1048576
  68.5 0.8 %copy.9 = f32[32,32,128]{2,1,0:T(8,128)} copy(f32[32,32,128]{2,1,0:T(8,128)S(1)} %get-tuple-element.3) | data formatting | bytes 1048576

commit v5 on v4

--- a/solution.py
+++ b/solution.py
@@ -182,7 +182,7 @@
             )
 
         def start():
-            for d, (dx, dy) in enumerate(dirs):
+            for d, (dx, dy) in sorted(enumerate(dirs), key=lambda i: -abs(i[1][0]) - abs(i[1][1])):
                 @pl.when(exists(dx, dy))
                 def _():
                     copy(d, dx, dy).start()
@@ -450,13 +450,6 @@
     for p in range(16):
         l, m = pair_of(p)
         re1[2 * p : 2 * p + 2, :] = rows[m - 1, 2 * l : 2 * l + 2, :]
-    for l in range(1, 5):
-        clear2(S[l])
-        clear2(M[l])
-    for name in MESSAGES:
-        if name not in ("f0", "g1", "f1"):
-            clear(r_["in_" + name])
-
     def side_phi(i, c):
         S0[1, 4 + i, 0:8, :] = jnp.zeros((8, 128), f32)
         S0[1, 4 + i, 40:48, :] = jnp.zeros((8, 128), f32)
@@ -832,6 +825,7 @@
     powers(2, t2, t3, t4)
     for l in (1, 2, 3):
         square(l)
+    clear(r_["in_s2"])
 
     def both0(h, x, v):
         bb0[0, x] = 0.8192 * t3[0, x] + 0.4096 * v
@@ -844,6 +838,10 @@
     y1_start()
     stencil(0, t4, both0, 3, lambda h, x, v: v, (0,))
     stencil(0, bb0, into(cc0), 2, lambda h, x, v: (0.1536 if h else 0.9728) * t2[0, x] + v)
+    for r in (S3, S4, M3, M4):
+        clear2(r)
+    for name in ("s3", "s4", "m3", "m2", "m1"):
+        clear(r_["in_" + name])
     x1_finish()
     y1_finish()
     residual(1)

time: 69.4 us -> 68.7 us (0.990)
  Pallas kernels: 67.1 us -> 66.3 us
    pallas_call x1, Pallas kernels: 67.1 us -> 66.3 us  [body(): pl.pallas_call(lambda *r: kernel(sizes, *r), out_shape=(pltpu.VMEM(n, f32...]
where the time goes in v5:
time: 68.7 us; the launch traced here: 68.5 us
  Pallas kernels  66.3 us (97%)
  local copies, waits for them, and re-layouts  1.59 us (2%)
    pallas_call x1, Pallas kernels, body(): pl.pallas_call(lambda *r: kernel(sizes, *r), out_shape=(pltpu.VMEM(n, f32...  66.3 us
    unnamed x2, local copies, waits for them, and re-layouts  1.59 us

profile of v5, /device:TPU:2, one launch (start us, length us, event | category | flops | bytes accessed | tf_op | source)
XLA Modules:
  0.0 68.5 jit_solution(14959326989062625561)
XLA Ops:
  0.6 66.3 %vcycle.1 = (f32[32,32,128]{2,1,0:T(8,128)S(1)}, f32[32,32,128]{2,1,0:T(8,128)S(1)}) custom-call(f32[32,32,128]{2,1,0:T(8,128)} %r_0_.1, f32[1,128]{1,0:T(1,128)} %bitcast.1, f32[5,128,128]{2,1,0:T(8,128)} %r_2_.1, f32[5]{0:T(128)} %r_3_.1), custom_call_target="tpu_custom_call" | custom-call | tf_op jit(solution)/shard_map/vcycle/pallas_call | solution.py:954
  66.9 0.8 %copy.8 = f32[32,32,128]{2,1,0:T(8,128)} copy(f32[32,32,128]{2,1,0:T(8,128)S(1)} %get-tuple-element.2) | data formatting | bytes 1048576
  67.7 0.8 %copy.9 = f32[32,32,128]{2,1,0:T(8,128)} copy(f32[32,32,128]{2,1,0:T(8,128)S(1)} %get-tuple-element.3) | data formatting | bytes 1048576

commit v6 on v5

--- a/solution.py
+++ b/solution.py
@@ -548,9 +548,13 @@
         wr = iota((128, width), 0)
         mrow = ((wr & 15) - 11) if level == 0 else lm_of(wr & 15)[1]
         out = jnp.zeros((128, width), f32)
+        pb, eb = pick_rows.astype(bf16), expand.astype(bf16)
+        vh, vl = split(jnp.concatenate(VS, 1))
+        y = mm(pb, vh) + mm(pb, vl)
+        yh, yl = split(jnp.concatenate([y[:, 128 * n : 128 * n + 128] for n in range(4)], 0))
+        x = mm(yh, eb) + mm(yl, eb)
         for n in range(4):
-            x = dot3(dot3(pick_rows, VS[n]), expand)
-            out = out + jnp.where(mrow - mc == n, x, 0.0)
+            out = out + jnp.where(mrow - mc == n, x[128 * n : 128 * n + 128], 0.0)
         return out
 
     L0 = funct(0)

time: 68.7 us -> 68.5 us (level)
  no operation moved by 1% of the time
where the time goes in v6:
time: 68.5 us; the launch traced here: 68.3 us
  Pallas kernels  66.1 us (96%)
  local copies, waits for them, and re-layouts  1.59 us (2%)
    pallas_call x1, Pallas kernels, body(): pl.pallas_call(lambda *r: kernel(sizes, *r), out_shape=(pltpu.VMEM(n, f32...  66.1 us
    unnamed x2, local copies, waits for them, and re-layouts  1.59 us

profile of v6, /device:TPU:2, one launch (start us, length us, event | category | flops | bytes accessed | tf_op | source)
XLA Modules:
  0.0 68.3 jit_solution(11452871633250360634)
XLA Ops:
  0.6 66.1 %vcycle.1 = (f32[32,32,128]{2,1,0:T(8,128)S(1)}, f32[32,32,128]{2,1,0:T(8,128)S(1)}) custom-call(f32[32,32,128]{2,1,0:T(8,128)} %r_0_.1, f32[1,128]{1,0:T(1,128)} %bitcast.1, f32[5,128,128]{2,1,0:T(8,128)} %r_2_.1, f32[5]{0:T(128)} %r_3_.1), custom_call_target="tpu_custom_call" | custom-call | tf_op jit(solution)/shard_map/vcycle/pallas_call | solution.py:958
  66.7 0.8 %copy.8 = f32[32,32,128]{2,1,0:T(8,128)} copy(f32[32,32,128]{2,1,0:T(8,128)S(1)} %get-tuple-element.2) | data formatting | bytes 1048576
  67.5 0.8 %copy.9 = f32[32,32,128]{2,1,0:T(8,128)} copy(f32[32,32,128]{2,1,0:T(8,128)S(1)} %get-tuple-element.3) | data formatting | bytes 1048576
